TPU v7x, 256 devices: a whole 4x4x8 slice. The times are simulated.
256 devices in a mesh: ep: 64 (over z, x, core), tp: 4 (over y).
Axes of the slice: x: 4, y: 4, z: 8, core: 2. Of those that a mesh axis runs over, the one named last changes fastest.
Arguments:
- tokens: bfloat16 [16384, 2048], P('ep', 'tp'), may hold values from -180 to 180
- norm_gain: float32 [2048], replicated, may hold values from 0.1 to 1.9
- router_weight: bfloat16 [2048, 60], P('tp'), may hold values from -2 to 2
- shared_gate_w: bfloat16 [2048], replicated, may hold values from -0.125 to 0.125
- expert_ids: int32 [16384, 4], P('ep'), may hold values from 0 to 59, all different within a row; in each aligned block of 256 rows (0 to 255, 256 to 511, ...) at most 32 rows name the same one
- w_gate: bfloat16 [64, 2048, 1408], P('ep', None, 'tp'), may hold values from -0.125 to 0.125
- w_up: bfloat16 [64, 2048, 1408], P('ep', None, 'tp'), may hold values from -0.125 to 0.125
- w_down: bfloat16 [64, 1408, 2048], P('ep', 'tp'), may hold values from -1.5 to 1.5
- shared_w_gate: bfloat16 [2048, 2816], P(None, 'tp'), may hold values from -0.125 to 0.125
- shared_w_up: bfloat16 [2048, 2816], P(None, 'tp'), may hold values from -0.125 to 0.125
- shared_w_down: bfloat16 [2816, 2048], P('tp'), may hold values from -0.109375 to 0.109375
Outputs:
- moe_out: bfloat16 [16384, 2048], P('ep', 'tp')
Inputs may be any that keep to these rules, and one draw needn't show every extreme that they name: `expert_ids`: each row names 4 different experts below 60. Within the 256 rows of one index of ep no expert is named by more than 32 rows, and in some of these blocks one expert is named by exactly 32 rows.
All inputs are finite; a program needn't handle non-finite values.
Results may differ from a plain program's by a relative error of at most 0.0069.
Values may be sent and summed in bfloat16 or wider, within the bound.
No kernel may reach another device: no remote copies, remote signals or barrier semaphores. Data moves between devices by JAX's collectives and lax.ppermute only.
A program may use at most 128 MiB of HBM per device.

v0:
```python
import jax
import jax.numpy as jnp
from jax import lax
from jax.sharding import PartitionSpec as P


def laid_out(parts, dim):
    lengths = list(parts.shape[1:])
    lengths[dim] *= parts.shape[0]
    return jnp.moveaxis(parts, 0, dim).reshape(lengths)


def copy_for_each(value, axis):
    peers = lax.axis_size(axis)
    return lax.all_to_all(
        jnp.broadcast_to(value[None], (peers, *value.shape)), axis, 0, 0, tiled=True
    )


def collect(value, axis, dim):
    return laid_out(copy_for_each(value, axis), dim)


def taken_together(value, axis):
    return copy_for_each(value, axis).sum(axis=0)


def turned_gather(arrays, axis, dims):
    turned = [jnp.moveaxis(a, dim, 0) for a, dim in zip(arrays, dims)]
    both = jnp.concatenate([t.reshape(len(t), -1) for t in turned], axis=1)
    out, at, done = (lax.all_gather(both, axis, axis=0, tiled=True), 0, [])
    for t, dim in zip(turned, dims):
        piece = out[:, at : at + t[0].size].reshape(-1, *t.shape[1:])
        done.append(jnp.moveaxis(piece, 0, dim))
        at += t[0].size
    return tuple(done)


def cut_along(value, dim, peers):
    before, after = (value.shape[:dim], value.shape[dim + 1 :])
    return jnp.moveaxis(value.reshape(*before, peers, -1, *after), dim, 0)


def sent_and_summed(value, axis, dim):
    peers = lax.axis_size(axis)
    parts = lax.all_to_all(cut_along(value, dim, peers), axis, 0, 0, tiled=True)
    return jnp.sum(parts.astype(jnp.float32), axis=0)


def send_back(summed):
    return lax.all_to_all(summed, "ep", split_axis=0, concat_axis=0, tiled=True)


def expert_rows(arrived, w_gate, w_up, w_down):
    share = arrived.shape[0] // lax.axis_size("tp")
    mine = lax.dynamic_slice_in_dim(arrived, lax.axis_index("tp") * share, share, 0)
    gate_act = jnp.einsum("sekd,edf->sekf", mine, w_gate, preferred_element_type=jnp.float32)
    up_act = jnp.einsum("sekd,edf->sekf", mine, w_up, preferred_element_type=jnp.float32)
    hidden = (jax.nn.silu(gate_act) * up_act).astype(jnp.bfloat16)
    full_out = jnp.einsum(
        "sekf,efd->sekd", hidden, w_down, preferred_element_type=jnp.float32
    ).astype(jnp.bfloat16)
    summed = lax.all_to_all(full_out, "tp", split_axis=3, concat_axis=0, tiled=True)
    return send_back(summed)


def per_device(
    tokens,
    norm_gain,
    router_weight,
    shared_gate_w,
    expert_ids,
    w_gate,
    w_up,
    w_down,
    shared_w_gate,
    shared_w_up,
    shared_w_down,
):
    width = tokens.shape[1]
    tok_rows = tokens.shape[0]
    column_start = lax.axis_index("tp") * width
    whole = collect(tokens, "tp", 1)
    values = whole.astype(jnp.float32)
    inv_rms = lax.rsqrt(jnp.mean(values * values, axis=-1, keepdims=True) + 1e-06)
    normed = (values * inv_rms * norm_gain[None, :]).astype(jnp.bfloat16)
    own_part = lax.dynamic_slice_in_dim(normed, column_start, width, 1)
    partial_logits = jnp.dot(own_part, router_weight, preferred_element_type=jnp.float32)
    logits = taken_together(partial_logits, "tp")
    probs = jax.nn.softmax(logits, axis=-1)
    expert_count = logits.shape[1]
    matches = expert_ids[:, :, None] == jnp.arange(expert_count, dtype=jnp.int32)[None, None, :]
    route_weight = jnp.sum(jnp.where(matches, probs[:, None, :], 0.0), axis=-1)
    gate_whole, up_whole = turned_gather((w_gate, w_up), "tp", (2, 2))
    down_whole = lax.all_gather(w_down, "tp", axis=1, tiled=True)
    experts_here = w_gate.shape[0]
    slot_count = lax.axis_size("ep") * experts_here
    capacity = tok_rows // 8
    flat_ids = expert_ids.reshape(-1)
    one_hot = (flat_ids[:, None] == jnp.arange(slot_count, dtype=jnp.int32)[None, :]).astype(
        jnp.int32
    )
    before = jnp.cumsum(one_hot, axis=0) - one_hot
    order_rank = jnp.sum(before * one_hot, axis=1)
    slot_ids = (flat_ids * capacity + order_rank).reshape(expert_ids.shape)
    targets = jnp.arange(slot_count * capacity, dtype=jnp.int32)
    dispatch_map = jnp.sum(
        (slot_ids[None, :, :] == targets[:, None, None]).astype(jnp.bfloat16), axis=2
    )
    outgoing = jnp.dot(dispatch_map, normed, preferred_element_type=jnp.float32).astype(
        jnp.bfloat16
    )
    outgoing = outgoing.reshape(lax.axis_size("ep"), experts_here, capacity, normed.shape[1])
    returned = expert_rows(
        lax.all_to_all(outgoing, "ep", split_axis=0, concat_axis=0, tiled=True),
        w_gate=gate_whole,
        w_up=up_whole,
        w_down=down_whole,
    )
    picked = returned.reshape(slot_count * capacity, width)[slot_ids]
    routed = jnp.sum(route_weight[:, :, None] * picked.astype(jnp.float32), axis=1)
    shared_gate_act = jnp.dot(normed, shared_w_gate, preferred_element_type=jnp.float32)
    shared_up_act = jnp.dot(normed, shared_w_up, preferred_element_type=jnp.float32)
    shared_hidden = (jax.nn.silu(shared_gate_act) * shared_up_act).astype(jnp.bfloat16)
    shared_part = jnp.dot(shared_hidden, shared_w_down, preferred_element_type=jnp.float32)
    shared_own = sent_and_summed(shared_part.astype(jnp.bfloat16), "tp", 1)
    share_gate = jax.nn.sigmoid(jnp.dot(normed, shared_gate_w, preferred_element_type=jnp.float32))
    return (share_gate[:, None] * shared_own + routed).astype(jnp.bfloat16)


def solution(mesh):
    return jax.shard_map(
        per_device,
        mesh=mesh,
        in_specs=(
            P("ep", "tp"),
            P(),
            P("tp", None),
            P(),
            P("ep", None),
            P("ep", None, "tp"),
            P("ep", None, "tp"),
            P("ep", "tp", None),
            P(None, "tp"),
            P(None, "tp"),
            P("tp", None),
        ),
        out_specs=P("ep", "tp"),
        check_vma=False,
    )
```

profile of v0, /device:TPU:8, one launch (start us, length us, event | category | flops | bytes accessed | tf_op | source)
XLA Modules:
  0.0 429.5 jit_solution(3899483268526843282)
XLA Ops:
  12.5 6.4 %all-to-all-start = ((bf16[4,256,512]{1,2,0:T(8,128)(2,1)}), bf16[4,256,512]{1,2,0:T(8,128)(2,1)}, u32[]{:S(2)}, u32[]{:S(2)}) async-start(bf16[4,256,512]{1,2,0:T(8,128)(2,1)} %broadcast_in_dim.14), calls=%async_computation | async-start | bytes 2097152 | tf_op jit(solution)/shard_map/all_to_all | solution.py:15
  19.2 18.0 %reduce-window.6 = s32[64,8,128]{2,1,0:T(8,128)S(1)} reduce-window(s32[64,8,128]{2,1,0:T(8,128)S(1)} %fusion.47, s32[]{:T(128)} %constant.8.clone.1), window={size=1x1x128 pad=0_0x0_0x127_0}, to_apply=%region_6.7 | reduce-window | flops 8323072 | bytes 524292 | tf_op jit(solution)/shard_map/reduce-window
  43.9 5.8 %convolution_convert_fusion = bf16[2048,2048]{1,0:T(8,128)(2,1)} fusion(bf16[2048,256]{1,0:T(8,128)(2,1)S(1)} %copy-done.2, bf16[256,2048]{0,1:T(8,128)(2,1)S(1)} %fusion.32), kind=kOutput, calls=%fused_computation.3 | convolution fusion | flops 2151677952 | bytes 10485760 | tf_op jit(solution)/shard_map/dot_general | solution.py:110
  49.7 10.9 %all-to-all-start.3 = ((bf16[64,1,32,2048]{3,2,1,0:T(8,128)(2,1)}), bf16[64,1,32,2048]{3,2,1,0:T(8,128)(2,1)}, u32[]{:S(2)}, u32[]{:S(2)}) async-start(bf16[64,1,32,2048]{3,2,1,0:T(8,128)(2,1)} %bitcast.131), calls=%async_computation.3 | async-start | bytes 16777216 | tf_op jit(solution)/shard_map/all_to_all | solution.py:115
  62.5 63.2 %all-gather.3.cloned.1.call-done = bf16[1408,4096]{1,0:T(8,128)(2,1)} async-done(((bf16[352,4096]{1,0:T(8,128)(2,1)}), bf16[1408,4096]{1,0:T(8,128)(2,1)}) %all-gather.3.cloned.1.call-update) | async-done | bytes 11534352 | tf_op jit(solution)/shard_map/all_gather | solution.py:31
  125.7 11.0 %fusion.56 = (bf16[1408,2048]{1,0:T(8,128)(2,1)}, bf16[1408,2048]{1,0:T(8,128)(2,1)}) fusion(bf16[1408,4096]{1,0:T(8,128)(2,1)} %all-gather.3.cloned.1.call-done), kind=kLoop, calls=%fused_computation.61 | loop fusion | bytes 23068672 | tf_op jit(solution)/shard_map/slice | solution.py:33
  136.6 8.5 %copy.110 = bf16[1408,2048]{0,1:T(8,128)(2,1)} copy(bf16[1408,2048]{1,0:T(8,128)(2,1)} %get-tuple-element.7) | data formatting | bytes 11534336
  145.2 8.4 %copy.111 = bf16[1408,2048]{0,1:T(8,128)(2,1)} copy(bf16[1408,2048]{1,0:T(8,128)(2,1)} %get-tuple-element.8) | data formatting | bytes 11534336
  153.5 93.2 %all-to-all-done.3 = bf16[64,1,32,2048]{3,2,1,0:T(8,128)(2,1)} async-done(((bf16[64,1,32,2048]{3,2,1,0:T(8,128)(2,1)}), bf16[64,1,32,2048]{3,2,1,0:T(8,128)(2,1)}, u32[]{:S(2)}, u32[]{:S(2)}) %all-to-all-start.3) | async-done | bytes 8388640 | tf_op jit(solution)/shard_map/all_to_all | solution.py:115
  247.5 4.8 %all-to-all-start.2 = ((f32[4,256,60]{1,2,0:T(8,128)}), f32[4,256,60]{1,2,0:T(8,128)S(1)}, u32[]{:S(2)}, u32[]{:S(2)}) async-start(f32[4,256,60]{1,2,0:T(8,128)} %broadcast_in_dim.15), calls=%async_computation.2 | async-start | bytes 524288 | tf_op jit(solution)/shard_map/all_to_all | solution.py:15
  252.3 8.3 %fusion.8 = f32[16,1,32,1408]{3,2,0,1:T(8,128)} fusion(bf16[1408,2048]{0,1:T(8,128)(2,1)} %copy.110, bf16[64,1,32,2048]{3,2,1,0:T(8,128)(2,1)} %all-to-all-done.3, s32[]{:T(128)S(6)} %select_n.15), kind=kOutput, calls=%fused_computation.11 | convolution fusion | flops 2952790016 | bytes 10747908 | tf_op jit(solution)/shard_map/sekd,edf->sekf/dot_general | solution.py:57
  260.6 14.2 %fusion.23 = bf16[16,1,32,2048]{3,2,0,1:T(8,128)(2,1)} fusion(bf16[1,1408,2048]{2,1,0:T(8,128)(2,1)} %all-gather.5.cloned.1.call-done, bf16[1408,2048]{0,1:T(8,128)(2,1)} %copy.111, f32[16,1,32,1408]{3,2,0,1:T(8,128)} %fusion.8, bf16[64,1,32,2048]{3,2,1,0:T(8,128)(2,1)} %all-to-all-done.3, s32[]{:T(128)S(6)} %select_n.15), kind=kOutput, calls=%fused_computation.17 | convolution fusion | flops 5910953984 | bytes 18612228 | tf_op jit(solution)/shard_map/sekf,efd->sekd/dot_general | solution.py:60
  274.8 9.9 %copy.104 = bf16[16,1,32,2048]{2,0,1,3:T(8,128)(2,1)} copy(bf16[16,1,32,2048]{3,2,0,1:T(8,128)(2,1)} %fusion.23) | data formatting | bytes 4194304 | tf_op jit(solution)/shard_map/convert_element_type | solution.py:62
  284.7 10.6 %reshape.141 = bf16[4,2,131072]{2,1,0:T(2,128)(2,1)} reshape(bf16[2048,1,16,32]{3,2,1,0:T(8,128)(2,1)} %bitcast.132) | data formatting | bytes 4194304
  295.3 4.8 %all-to-all-start.4 = ((bf16[4,2,131072]{2,1,0:T(2,128)(2,1)}), bf16[4,2,131072]{2,1,0:T(2,128)(2,1)}, u32[]{:S(2)}, u32[]{:S(2)}) async-start(bf16[4,2,131072]{2,1,0:T(2,128)(2,1)} %reshape.141), calls=%async_computation.4 | async-start | bytes 4194304 | tf_op jit(solution)/shard_map/all_to_all | solution.py:63
  300.1 3.9 fusion.58
  304.0 6.5 %convolution_convert_fusion.1 = bf16[256,2048]{1,0:T(8,128)(2,1)} fusion(bf16[704,2048]{1,0:T(8,128)(2,1)S(1)} %copy-done, bf16[2048,704]{0,1:T(8,128)(2,1)} %param.20, bf16[256,2048]{0,1:T(8,128)(2,1)} %copy-done.1, f32[256,704]{0,1:T(8,128)} %fusion.58), kind=kOutput, calls=%fused_computation.19 | convolution fusion | flops 1478000640 | bytes 8585216 | tf_op jit(solution)/shard_map/dot_general | solution.py:125
  312.9 8.3 %all-to-all-done.4 = bf16[4,2,131072]{2,1,0:T(2,128)(2,1)} async-done(((bf16[4,2,131072]{2,1,0:T(2,128)(2,1)}), bf16[4,2,131072]{2,1,0:T(2,128)(2,1)}, u32[]{:S(2)}, u32[]{:S(2)}) %all-to-all-start.4) | async-done | bytes 2097184 | tf_op jit(solution)/shard_map/all_to_all | solution.py:63
  321.1 5.7 %all-to-all-start.1 = ((bf16[4,256,512]{2,1,0:T(8,128)(2,1)}), bf16[4,256,512]{2,1,0:T(8,128)(2,1)}, u32[]{:S(2)}, u32[]{:S(2)}) async-start(bf16[4,256,512]{2,1,0:T(8,128)(2,1)} %bitcast.136), calls=%async_computation.1 | async-start | bytes 2097152 | tf_op jit(solution)/shard_map/all_to_all | solution.py:46
  326.8 7.4 %reshape.142 = bf16[2048,1,16,32]{3,2,1,0:T(8,128)(2,1)} reshape(bf16[4,2,131072]{2,1,0:T(2,128)(2,1)} %all-to-all-done.4) | data formatting | bytes 4194304
  334.2 9.9 %copy.109 = bf16[16,1,32,4,512]{4,3,2,0,1:T(4,128)(2,1)} copy(bf16[16,1,32,4,512]{2,0,4,3,1:T(8,128)(2,1)} %bitcast.133) | data formatting | bytes 4194304 | tf_op jit(solution)/shard_map/all_to_all | solution.py:63
  347.6 10.4 %all-to-all-start.5 = ((bf16[64,1,32,512]{3,2,1,0:T(8,128)(2,1)}), bf16[64,1,32,512]{3,2,1,0:T(8,128)(2,1)}, u32[]{:S(2)}, u32[]{:S(2)}) async-start(bf16[64,1,32,512]{3,2,1,0:T(8,128)(2,1)} %bitcast.135), calls=%async_computation.5 | async-start | bytes 4194304 | tf_op jit(solution)/shard_map/all_to_all | solution.py:51
  361.6 47.6 %all-to-all-done.5 = bf16[64,1,32,512]{3,2,1,0:T(8,128)(2,1)} async-done(((bf16[64,1,32,512]{3,2,1,0:T(8,128)(2,1)}), bf16[64,1,32,512]{3,2,1,0:T(8,128)(2,1)}, u32[]{:S(2)}, u32[]{:S(2)}) %all-to-all-start.5) | async-done | bytes 2097184 | tf_op jit(solution)/shard_map/all_to_all | solution.py:51
  409.1 7.0 %gather_fusion = bf16[1024,512]{1,0:T(8,128)(2,1)} fusion(bf16[2048,512]{1,0:T(8,128)(2,1)} %bitcast.36, s32[1024]{0:T(1024)S(1)} %broadcast_clamp_fusion), kind=kCustom, calls=%fused_computation | custom fusion | bytes 2101248 | tf_op jit(solution)/shard_map/gather | solution.py:120
  (65 shorter events, 31.4 us)
Async XLA Ops:
  6.5 297.4 %copy-start = (bf16[704,2048]{1,0:T(8,128)(2,1)S(1)}, bf16[704,2048]{1,0:T(8,128)(2,1)}, u32[]{:S(2)}) copy-start(bf16[704,2048]{1,0:T(8,128)(2,1)} %param.21) | copy-start | bytes 8650756
  6.5 119.1 %all-gather.3.cloned.1.call-start = ((), (), s32[]{:S(2)}) async-start(), calls=%async_computation.6 | async-start | bytes 14417920 | tf_op jit(solution)/shard_map/all_gather | solution.py:31
  10.3 0.9 copy-start.3
  10.4 8.5 %copy-start.5 = (s32[256,4]{0,1:T(4,128)S(1)}, s32[256,4]{0,1:T(4,128)}, u32[]{:S(2)}) copy-start(s32[256,4]{0,1:T(4,128)} %param.15) | copy-start | bytes 12292
  12.5 28.2 %all-to-all-start = ((bf16[4,256,512]{1,2,0:T(8,128)(2,1)}), bf16[4,256,512]{1,2,0:T(8,128)(2,1)}, u32[]{:S(2)}, u32[]{:S(2)}) async-start(bf16[4,256,512]{1,2,0:T(8,128)(2,1)} %broadcast_in_dim.14), calls=%async_computation | async-start | bytes 2097152 | tf_op jit(solution)/shard_map/all_to_all | solution.py:15
  18.8 23.5 %copy-start.6 = (f32[2048]{0:T(1024)S(1)}, f32[2048]{0:T(1024)}, u32[]{:S(2)}) copy-start(f32[2048]{0:T(1024)} %param.12) | copy-start | bytes 24580
  40.7 3.2 copy-start.2
  43.9 5.8 %copy-start.1 = (bf16[256,2048]{0,1:T(8,128)(2,1)}, bf16[256,2048]{0,1:T(8,128)(2,1)S(1)}, u32[]{:S(2)}) copy-start(bf16[256,2048]{0,1:T(8,128)(2,1)S(1)} %fusion.32) | copy-start | bytes 3145732
  49.7 11.7 %copy-start.4 = (bf16[512,60]{0,1:T(8,128)(2,1)S(1)}, bf16[512,60]{0,1:T(8,128)(2,1)}, u32[]{:S(2)}) copy-start(bf16[512,60]{0,1:T(8,128)(2,1)} %param.13) | copy-start | bytes 184324
  49.7 197.1 %all-to-all-start.3 = ((bf16[64,1,32,2048]{3,2,1,0:T(8,128)(2,1)}), bf16[64,1,32,2048]{3,2,1,0:T(8,128)(2,1)}, u32[]{:S(2)}, u32[]{:S(2)}) async-start(bf16[64,1,32,2048]{3,2,1,0:T(8,128)(2,1)} %bitcast.131), calls=%async_computation.3 | async-start | bytes 16777216 | tf_op jit(solution)/shard_map/all_to_all | solution.py:115
  60.6 200.0 %all-gather.5.cloned.1.call-start = ((), (), s32[]{:S(2)}) async-start(), calls=%async_computation.7 | async-start | bytes 7208960 | tf_op jit(solution)/shard_map/all_gather | solution.py:95
  247.5 47.8 %all-to-all-start.2 = ((f32[4,256,60]{1,2,0:T(8,128)}), f32[4,256,60]{1,2,0:T(8,128)S(1)}, u32[]{:S(2)}, u32[]{:S(2)}) async-start(f32[4,256,60]{1,2,0:T(8,128)} %broadcast_in_dim.15), calls=%async_computation.2 | async-start | bytes 524288 | tf_op jit(solution)/shard_map/all_to_all | solution.py:15
  295.3 25.9 %all-to-all-start.4 = ((bf16[4,2,131072]{2,1,0:T(2,128)(2,1)}), bf16[4,2,131072]{2,1,0:T(2,128)(2,1)}, u32[]{:S(2)}, u32[]{:S(2)}) async-start(bf16[4,2,131072]{2,1,0:T(2,128)(2,1)} %reshape.141), calls=%async_computation.4 | async-start | bytes 4194304 | tf_op jit(solution)/shard_map/all_to_all | solution.py:63
  321.1 26.4 %all-to-all-start.1 = ((bf16[4,256,512]{2,1,0:T(8,128)(2,1)}), bf16[4,256,512]{2,1,0:T(8,128)(2,1)}, u32[]{:S(2)}, u32[]{:S(2)}) async-start(bf16[4,256,512]{2,1,0:T(8,128)(2,1)} %bitcast.136), calls=%async_computation.1 | async-start | bytes 2097152 | tf_op jit(solution)/shard_map/all_to_all | solution.py:46
  347.6 10.6 %copy-start.7 = (bf16[2048]{0:T(1024)(128)(2,1)S(1)}, bf16[2048]{0:T(1024)(128)(2,1)}, u32[]{:S(2)}) copy-start(bf16[2048]{0:T(1024)(128)(2,1)} %param.14) | copy-start | bytes 12292
  347.6 61.6 %all-to-all-start.5 = ((bf16[64,1,32,512]{3,2,1,0:T(8,128)(2,1)}), bf16[64,1,32,512]{3,2,1,0:T(8,128)(2,1)}, u32[]{:S(2)}, u32[]{:S(2)}) async-start(bf16[64,1,32,512]{3,2,1,0:T(8,128)(2,1)} %bitcast.135), calls=%async_computation.5 | async-start | bytes 4194304 | tf_op jit(solution)/shard_map/all_to_all | solution.py:51
Sparse Core Ops, SparseCore 0:
  10.5 115.1 all-gather.2
  127.5 64.4 all-gather.4
where the time goes:
time: 431 us; the launch traced here: 429 us
  waiting for transfers between devices  213 us (49%)
  local copies, waits for them, and re-layouts  85.4 us (20%)
  starting transfers between devices  42.9 us (10%)
  matrix products  41.3 us (10%)
  other arithmetic  33.3 us (8%)
  between operations  13.6 us (3%)
    all_to_all x1, waiting for transfers between devices, per_device(): lax.all_to_all(outgoing, 'ep', split_axis=0, concat_axis=0, tiled=True)  93.2 us
    all_gather x1, waiting for transfers between devices, turned_gather(): out, at, done = (lax.all_gather(both, axis, axis=0, tiled=True), 0, [])  63.2 us
    all_to_all x1, waiting for transfers between devices, send_back(): return lax.all_to_all(summed, 'ep', split_axis=0, concat_axis=0, tiled=True)  47.6 us
    unnamed x23, local copies, waits for them, and re-layouts  36.1 us
    another operation x3, other arithmetic  18.2 us
    dot_general x1, matrix products, expert_rows(): jnp.einsum('sekf,efd->sekd', hidden, w_down, preferred_element_type=jnp.f...  14.2 us
    all_to_all x2, local copies, waits for them, and re-layouts, expert_rows(): lax.all_to_all(full_out, 'tp', split_axis=3, concat_axis=0, tiled=True)  13.4 us
    all_to_all x2, starting transfers between devices, copy_for_each(): lax.all_to_all(jnp.broadcast_to(value[None], (peers, *value.shape)), axis...  11.2 us
  transfers between devices with their start and end apart: 8, of which 4 were waited for; matrix products, arithmetic and copies ran while one was open for 33% of the time, Pallas kernels for 0%

commit v1 on v0

v1 whole, which is shorter than its diff:
```python
import jax
import jax.numpy as jnp
from jax import lax
from jax.experimental import pallas as pl
from jax.experimental.pallas import tpu as pltpu
from jax.sharding import PartitionSpec as P


BF16 = jnp.bfloat16
F32 = jnp.float32
BOTH = ("ep", "tp")
CHUNKS = 2


def pair_perms(mesh):
    ep, tp = mesh.shape["ep"], mesh.shape["tp"]
    near, across = [], []
    for e in range(ep):
        for t in range(tp):
            flip, mirror = t ^ 1, tp - 1 - t
            a, b = (flip, mirror) if e % 2 == 0 else (mirror, flip)
            near.append((e * tp + t, e * tp + a))
            across.append((e * tp + t, e * tp + b))
    return near, across


def dot(a, b, dims=((1,), (0,))):
    return lax.dot_general(a, b, (dims, ((), ())), preferred_element_type=F32)


HBM = pl.BlockSpec(memory_space=pltpu.HBM)
VMEM = pl.BlockSpec(memory_space=pltpu.VMEM)
SMEM = pl.BlockSpec(memory_space=pltpu.SMEM)
BIG = pltpu.CompilerParams(vmem_limit_bytes=60 * 1024 * 1024)
SMALL = pltpu.CompilerParams(vmem_limit_bytes=24 * 1024 * 1024)


def load(pairs, sems):
    copies = [pltpu.make_async_copy(a, b, sems.at[i]) for i, (a, b) in enumerate(pairs)]
    for c in copies:
        c.start()
    return copies


def halves(refs, target):
    units = refs[0].shape[0]
    return [(r, target.at[pl.ds(i * units, units)]) for i, r in enumerate(refs)]


def ffn_kernel(gain, x_in, gate_a, gate_b, up_a, up_b, down_a, down_b, out, xv, x, gate_w, up_w, down_w, y, sems):
    pairs = [(x_in, xv), *halves((gate_a, gate_b), gate_w), *halves((up_a, up_b), up_w)]
    copies = load(pairs + halves((down_a, down_b), down_w), sems)
    rows, full = x.shape
    half = full // 2
    copies[0].wait()
    small = 32
    first = lax.broadcasted_iota(jnp.int32, (small // 8, 8, half), 1) < 4

    def norm_step(i, carry):
        at = pl.ds(pl.multiple_of(i * 2 * small, 2 * small), 2 * small)
        v = xv[at, :].astype(F32)
        shifted = pltpu.roll(v, 4, 0).reshape(small // 8, 2, 8, half)[:, 1]
        v = v.reshape(small // 8, 2, 8, half)
        lower = jnp.where(first, v[:, 0], shifted).reshape(small, half)
        upper = jnp.where(first, shifted, v[:, 1]).reshape(small, half)
        squares = jnp.sum(lower * lower, axis=-1, keepdims=True)
        squares = squares + jnp.sum(upper * upper, axis=-1, keepdims=True)
        inv_rms = lax.rsqrt(squares / full + 1e-06)
        to = pl.ds(pl.multiple_of(i * small, small), small)
        x[to, :half] = (lower * inv_rms * gain[:, :half]).astype(BF16)
        x[to, half:] = (upper * inv_rms * gain[:, half:]).astype(BF16)
        return carry

    lax.fori_loop(0, rows // small, norm_step, 0)
    for c in copies[1:3]:
        c.wait()
    gate = dot(x[...], gate_w[...], ((1,), (1,)))
    for c in copies[3:5]:
        c.wait()
    up = dot(x[...], up_w[...], ((1,), (1,)))
    hidden = (gate / (1.0 + jnp.exp(-gate)) * up).astype(BF16)
    for c in copies[5:]:
        c.wait()
    y[...] = dot(hidden, down_w[...])

    def out_step(i, carry):
        at = pl.ds(pl.multiple_of(i * small, small), small)
        lower, upper = y[at, :half], y[at, half:]
        lower_up = pltpu.roll(lower, small - 4, 0).reshape(small // 8, 8, half)
        upper_down = pltpu.roll(upper, 4, 0).reshape(small // 8, 8, half)
        lower, upper = lower.reshape(small // 8, 8, half), upper.reshape(small // 8, 8, half)
        even, odd = jnp.where(first, lower, upper_down), jnp.where(first, lower_up, upper)
        both = jnp.concatenate([even[:, None], odd[:, None]], axis=1).reshape(2 * small, half)
        to = pl.ds(pl.multiple_of(i * 2 * small, 2 * small), 2 * small)
        out[to, :] = both.astype(out.dtype)
        return carry

    lax.fori_loop(0, rows // small, out_step, 0)


def half_ffn(gain, x, weights, dtype):
    (rows, full), units = (x.shape[0] // 2, x.shape[1] * 2), 2 * weights[0].shape[0]
    return pl.pallas_call(
        ffn_kernel,
        out_shape=jax.ShapeDtypeStruct(x.shape, dtype),
        in_specs=[VMEM] + [HBM] * 7,
        out_specs=VMEM,
        scratch_shapes=[
            pltpu.VMEM(x.shape, BF16),
            pltpu.VMEM((rows, full), BF16),
            *[pltpu.VMEM((units, full), BF16)] * 3,
            pltpu.VMEM((rows, full), F32),
            pltpu.SemaphoreType.DMA((7,)),
        ],
        cost_estimate=pl.CostEstimate(
            flops=6 * rows * full * units,
            transcendentals=rows * units,
            bytes_accessed=2 * (3 * units * full + 2 * rows * full),
        ),
        compiler_params=BIG,
    )(gain, x, *weights)


def dispatch_kernel(starts, pick, part_0, part_1, part_2, part_3, whole, *outs):
    width = part_0.shape[1]
    rows, half = outs[0].shape
    for k, part in enumerate((part_0, part_1, part_2, part_3)):
        whole[:, pl.ds(pl.multiple_of(starts[k], width), width)] = part[...]
    upper_row = lax.broadcasted_iota(jnp.int32, (rows, width), 0) % 8 // 4
    for k, a, b in ((0, part_0, part_3), (1, part_1, part_2)):
        is_a = upper_row == starts[k] // half
        at = pl.ds(pl.multiple_of(starts[k] % half, width), width)
        for c, out in enumerate(outs):
            out[:, at] = jnp.where(is_a, dot(pick[c], a[...]), dot(pick[c], b[...])).astype(BF16)


def dispatched_rows(starts, pick, parts):
    tokens, width = parts[0].shape
    full, rows = width * len(parts), pick.shape[1]
    out = jax.ShapeDtypeStruct((rows, full // 2), BF16)
    return pl.pallas_call(
        dispatch_kernel,
        out_shape=[jax.ShapeDtypeStruct((tokens, full), BF16)] + [out] * CHUNKS,
        in_specs=[SMEM] + [VMEM] * 5,
        out_specs=[VMEM] * (1 + CHUNKS),
        cost_estimate=pl.CostEstimate(
            flops=2 * pick.size * full, transcendentals=0, bytes_accessed=8 * tokens * full
        ),
        compiler_params=SMALL,
    )(starts, pick, *parts)


def gather_kernel(mix_hi, mix_lo, rows, base, out):
    half = rows.shape[1]
    for h in range(2):
        at = slice(h * half, (h + 1) * half)
        out[:, at] = base[:, at] + dot(mix_hi[h], rows[...]) + dot(mix_lo[h], rows[...])


def gathered(mix_hi, mix_lo, rows, base):
    return pl.pallas_call(
        gather_kernel,
        out_shape=jax.ShapeDtypeStruct(base.shape, F32),
        in_specs=[VMEM] * 4,
        out_specs=VMEM,
        cost_estimate=pl.CostEstimate(
            flops=4 * mix_hi.size * rows.shape[1], transcendentals=0, bytes_accessed=8 * base.size
        ),
        compiler_params=SMALL,
    )(mix_hi, mix_lo, rows, base)


def combine_kernel(starts, mix_hi, mix_lo, rows, base, mine, near, across, diag):
    width, half = mine.shape[1], rows.shape[1]
    for k, out in ((3, diag), (2, across), (1, near), (0, mine)):
        h = starts[k] // half
        from_rows = pl.ds(pl.multiple_of(starts[k] % half, width), width)
        value = dot(mix_hi[h], rows[:, from_rows]) + dot(mix_lo[h], rows[:, from_rows])
        at = pl.ds(pl.multiple_of(starts[k], width), width)
        out[...] = (base[:, at] + value).astype(out.dtype)


def combined(starts, mix_hi, mix_lo, rows, base):
    tokens, full = base.shape
    return pl.pallas_call(
        combine_kernel,
        out_shape=[jax.ShapeDtypeStruct((tokens, full // 4), d) for d in (F32, F32, BF16, BF16)],
        in_specs=[SMEM] + [VMEM] * 4,
        out_specs=[VMEM] * 4,
        cost_estimate=pl.CostEstimate(
            flops=4 * mix_hi.size * full // 2, transcendentals=0, bytes_accessed=8 * tokens * full
        ),
        compiler_params=SMALL,
    )(starts, mix_hi, mix_lo, rows, base)


def make(mesh):
    near_pairs, across_pairs = pair_perms(mesh)

    def body(
        tokens,
        norm_gain,
        router_weight,
        shared_gate_w,
        expert_ids,
        w_gate,
        w_up,
        w_down,
        shared_w_gate,
        shared_w_up,
        shared_w_down,
    ):
        rows, width = tokens.shape
        peers = lax.axis_size("tp")
        slots = lax.axis_size("ep")
        full = width * peers
        share = rows // 8 // peers // CHUNKS
        me = lax.axis_index("tp")
        flip, mirror = me ^ 1, peers - 1 - me
        first_core = lax.axis_index("ep") % 2 == 0
        near = jnp.where(first_core, flip, mirror)
        across = jnp.where(first_core, mirror, flip)
        starts = jnp.stack([me, near, across, me ^ 2]).astype(jnp.int32) * width

        def to_near(value):
            return lax.ppermute(value, BOTH, near_pairs)

        def to_across(value):
            return lax.ppermute(value, BOTH, across_pairs)

        def all_parts(value):
            a, b = to_near(value), to_across(value)
            return [value, a, b, to_across(a)]

        parts = all_parts(tokens)
        own_w = (w_gate[0].T, w_up[0].T, w_down[0])
        weights = []
        for w in own_w:
            weights += [w, to_near(w)]

        experts = jnp.arange(slots, dtype=jnp.int32)
        named = jnp.any(expert_ids[:, :, None] == experts[None, None, :], axis=1)
        order = jnp.arange(rows, dtype=jnp.int32)
        earlier = (order[None, :] < order[:, None]).astype(BF16)
        before = dot(earlier, named.astype(BF16))
        key = jnp.where(named, before, -1.0).astype(BF16)
        lane = jnp.arange(slots * 2 * share, dtype=jnp.int32)
        spread = (experts[:, None] == lane[None, :] // (2 * share)).astype(BF16)
        chunk = jnp.arange(CHUNKS, dtype=jnp.int32)
        mine = ((me * CHUNKS + chunk[:, None]) * share + lane[None, :] % share).astype(F32)
        hit = dot(key, spread)[None] == mine[:, None, :]
        pick = (dot(spread, key, ((0,), (1,)))[None] == mine[:, :, None]).astype(BF16)

        whole, *outgoing = dispatched_rows(starts, pick, parts)

        values = whole.astype(F32)
        inv_rms = lax.rsqrt(jnp.mean(values * values, axis=-1, keepdims=True) + 1e-06)
        normed = (values * inv_rms * norm_gain[None, :]).astype(BF16)
        shared_gate_act = dot(normed, shared_w_gate)
        shared_up_act = dot(normed, shared_w_up)
        shared_hidden = (jax.nn.silu(shared_gate_act) * shared_up_act).astype(BF16)
        shared_part = dot(shared_hidden, shared_w_down)
        share_gate = jax.nn.sigmoid(dot(normed, shared_gate_w[:, None]))
        shared_part = lax.optimization_barrier(share_gate * shared_part)

        routers = all_parts(router_weight)
        logits = sum(
            dot(lax.dynamic_slice_in_dim(normed, starts[k], width, 1), r)
            for k, r in enumerate(routers)
        )
        probs = jax.nn.softmax(logits, axis=-1)
        probs = jnp.pad(probs, ((0, 0), (0, slots - probs.shape[1])))
        probs_hi = probs.astype(BF16)
        probs_lo = (probs - probs_hi.astype(F32)).astype(BF16)
        of_half = lane // share % 2 == jnp.arange(2, dtype=jnp.int32)[:, None]
        used = hit[:, None] & of_half[None, :, None, :]
        mix_hi = jnp.where(used, dot(probs_hi, spread)[None, None], 0.0).astype(BF16)
        mix_lo = jnp.where(used, dot(probs_lo, spread)[None, None], 0.0).astype(BF16)
        mixes = [(mix_hi[c], mix_lo[c]) for c in range(CHUNKS)]
        mixes = lax.optimization_barrier(mixes)

        gain = norm_gain[None, :]
        acc = shared_part
        for c in range(CHUNKS):
            there = outgoing[c].reshape(slots, 2 * share, full // 2)
            arrived = lax.all_to_all(there, "ep", 0, 0, tiled=True)
            arrived = arrived.reshape(outgoing[c].shape)
            arrived_far = to_across(arrived)
            sent = half_ffn(gain, arrived_far, weights, BF16)
            got = to_across(sent)
            kept = half_ffn(gain, arrived, weights, F32)
            out = (kept + got.astype(F32)).astype(BF16).reshape(there.shape)
            returned = lax.all_to_all(out, "ep", 0, 0, tiled=True)
            returned = returned.reshape(outgoing[c].shape)
            if c < CHUNKS - 1:
                acc = gathered(*mixes[c], returned, acc)
            else:
                total_me, total_near, for_across, for_diag = combined(starts, *mixes[c], returned, acc)
        came_near = to_across(for_diag)
        came_me = to_across(for_across)
        again = to_near((total_near + came_near.astype(F32)).astype(BF16))
        return (total_me + came_me.astype(F32) + again.astype(F32)).astype(BF16)

    return body


def solution(mesh):
    return jax.shard_map(
        make(mesh),
        mesh=mesh,
        in_specs=(
            P("ep", "tp"),
            P(),
            P("tp", None),
            P(),
            P("ep", None),
            P("ep", None, "tp"),
            P("ep", None, "tp"),
            P("ep", "tp", None),
            P(None, "tp"),
            P(None, "tp"),
            P("tp", None),
        ),
        out_specs=P("ep", "tp"),
        check_vma=False,
    )
```

time: 431 us -> 233 us (0.54)
  waiting for transfers between devices: 213 us -> 81 us
  local copies, waits for them, and re-layouts: 85.4 us -> 11.3 us
  Pallas kernels: 0 us -> 39.6 us
  matrix products: 41.3 us -> 17.5 us
  other arithmetic: 33.3 us -> 11.6 us
  starting transfers between devices: 42.9 us -> 61.9 us
  between operations: 13.6 us -> 7.71 us
    all_to_all x6 -> x4, waiting for transfers between devices: 149 us -> 42.8 us  [the longest x2 24.6 us: body(): arrived = lax.all_to_all(there, 'ep', 0, 0, tiled=True)]
    all_gather x2 -> x0, waiting for transfers between devices: 63.2 us -> none  [the longest x1 63.2 us: turned_gather(): out, at, done = (lax.all_gather(both, axis, axis=0, tiled=True), 0, [])]
    pallas_call x0 -> x7, Pallas kernels: none -> 39.6 us  [the longest x4 32.8 us: half_ffn(): pl.pallas_call(ffn_kernel, out_shape=jax.ShapeDtypeStruct(x.shape, dtype)...]
    ppermute x0 -> x16, waiting for transfers between devices: none -> 38.2 us  [the longest x6 25.6 us: to_near(): return lax.ppermute(value, BOTH, near_pairs)]
    unnamed x23 -> x31, local copies, waits for them, and re-layouts: 36.1 us -> 9.62 us
    dot_general x7 -> x12, matrix products: 41.3 us -> 17.5 us  [dot(): return lax.dot_general(a, b, (dims, ((), ())), preferred_element_type=F32)]
    ppermute x0 -> x16, starting transfers between devices: none -> 21.6 us  [the longest x10 10.8 us: to_across(): return lax.ppermute(value, BOTH, across_pairs)]
    another operation x3 -> x0, other arithmetic: 18.2 us -> none
  transfers between devices with their start and end apart: 8 -> 20, of which waited for: 4 -> 8; matrix products, arithmetic and copies ran while one was open for 33% -> 13% of each run, Pallas kernels for 0% -> 15%
where the time goes in v1:
time: 233 us; the launch traced here: 231 us
  waiting for transfers between devices  81 us (35%)
  starting transfers between devices  61.9 us (27%)
  Pallas kernels  39.6 us (17%)
  matrix products  17.5 us (8%)
  other arithmetic  11.6 us (5%)
  local copies, waits for them, and re-layouts  11.3 us (5%)
  between operations  7.71 us (3%)
    pallas_call x4, Pallas kernels, half_ffn(): pl.pallas_call(ffn_kernel, out_shape=jax.ShapeDtypeStruct(x.shape, dtype)...  32.8 us
    ppermute x6, waiting for transfers between devices, to_near(): return lax.ppermute(value, BOTH, near_pairs)  25.6 us
    all_to_all x2, waiting for transfers between devices, body(): arrived = lax.all_to_all(there, 'ep', 0, 0, tiled=True)  24.6 us
    all_to_all x2, starting transfers between devices, body(): returned = lax.all_to_all(out, 'ep', 0, 0, tiled=True)  22.5 us
    all_to_all x2, waiting for transfers between devices, body(): returned = lax.all_to_all(out, 'ep', 0, 0, tiled=True)  18.2 us
    all_to_all x2, starting transfers between devices, body(): arrived = lax.all_to_all(there, 'ep', 0, 0, tiled=True)  17.8 us
    dot_general x12, matrix products, dot(): return lax.dot_general(a, b, (dims, ((), ())), preferred_element_type=F32)  17.5 us
    ppermute x10, waiting for transfers between devices, to_across(): return lax.ppermute(value, BOTH, across_pairs)  12.7 us
  transfers between devices with their start and end apart: 20, of which 8 were waited for; matrix products, arithmetic and copies ran while one was open for 13% of the time, Pallas kernels for 15%

profile of v1, /device:TPU:8, one launch (start us, length us, event | category | flops | bytes accessed | tf_op | source)
XLA Modules:
  0.0 230.6 jit_solution(1872873541781150424)
XLA Ops:
  4.1 5.2 %collective-permute-done.part_1 = bf16[256,512]{1,0:T(8,128)(2,1)S(1)} collective-permute-done((bf16[256,512]{1,0:T(8,128)(2,1)}, bf16[256,512]{1,0:T(8,128)(2,1)S(1)}, u32[]{:S(2)}, u32[]{:S(2)}) %collective-permute-start) | collective-permute-done | bytes 262176 | tf_op jit(solution)/shard_map/ppermute | solution.py:226
  10.3 5.4 %collective-permute-done.2.part_3 = bf16[256,512]{1,0:T(8,128)(2,1)S(1)} collective-permute-done((bf16[256,512]{1,0:T(8,128)(2,1)S(1)}, bf16[256,512]{1,0:T(8,128)(2,1)S(1)}, u32[]{:S(2)}, u32[]{:S(2)}) %collective-permute-start.2) | collective-permute-done | bytes 262176 | tf_op jit(solution)/shard_map/ppermute | solution.py:229
  21.5 11.9 %all-to-all-start.2 = ((bf16[64,8,1024]{2,1,0:T(8,128)(2,1)}), bf16[64,8,1024]{2,1,0:T(8,128)(2,1)}, u32[]{:S(2)}, u32[]{:S(2)}) async-start(bf16[64,8,1024]{2,1,0:T(8,128)(2,1)} %bitcast.50), calls=%async_computation.2 | async-start | bytes 2097152 | tf_op jit(solution)/shard_map/all_to_all | solution.py:286
  37.5 24.6 %all-to-all-done.2 = bf16[64,8,1024]{2,1,0:T(8,128)(2,1)} async-done(((bf16[64,8,1024]{2,1,0:T(8,128)(2,1)}), bf16[64,8,1024]{2,1,0:T(8,128)(2,1)}, u32[]{:S(2)}, u32[]{:S(2)}) %all-to-all-start.2) | async-done | bytes 1048608 | tf_op jit(solution)/shard_map/all_to_all | solution.py:286
  71.1 5.9 %all-to-all-start = ((bf16[64,8,1024]{2,1,0:T(8,128)(2,1)}), bf16[64,8,1024]{2,1,0:T(8,128)(2,1)}, u32[]{:S(2)}, u32[]{:S(2)}) async-start(bf16[64,8,1024]{2,1,0:T(8,128)(2,1)} %bitcast.49), calls=%async_computation | async-start | bytes 2097152 | tf_op jit(solution)/shard_map/all_to_all | solution.py:286
  79.6 16.0 %collective-permute-done.3 = bf16[512,60]{0,1:T(8,128)(2,1)} collective-permute-done((bf16[512,60]{0,1:T(8,128)(2,1)S(1)}, bf16[512,60]{0,1:T(8,128)(2,1)}, u32[]{:S(2)}, u32[]{:S(2)}) %collective-permute-start.3) | collective-permute-done | bytes 61472 | tf_op jit(solution)/shard_map/ppermute | solution.py:226
  97.7 8.1 %shard_map.113 = bf16[512,1024]{1,0:T(8,128)(2,1)} custom-call(f32[1,2048]{1,0:T(1,128)} %bitcast.66, bf16[512,1024]{1,0:T(8,128)(2,1)} %collective-permute-done.11.x_in, bf16[352,2048]{1,0:T(8,128)(2,1)} %bitcast.52, bf16[352,2048]{1,0:T(8,128)(2,1)} %collective-permute-done.6.gate_b, bf16[352,2048]{1,0:T(8,128)(2,1)} %bitcast.57, ...), custom_call_target="tpu_custom_call" | custom-call | flops 2214592512 | bytes 10747904 | tf_op jit(solution)/shard_map/pallas_call | solution.py:103
  109.6 8.4 %shard_map.112 = f32[512,1024]{1,0:T(8,128)} custom-call(f32[1,2048]{1,0:T(1,128)} %bitcast.67, bf16[512,1024]{1,0:T(8,128)(2,1)} %bitcast.25.x_in, bf16[352,2048]{1,0:T(8,128)(2,1)} %bitcast.53, bf16[352,2048]{1,0:T(8,128)(2,1)} %collective-permute-done.6.gate_b, bf16[352,2048]{1,0:T(8,128)(2,1)} %bitcast.58, ...), custom_call_target="tpu_custom_call" | custom-call | flops 2214592512 | bytes 10747904 | tf_op jit(solution)/shard_map/pallas_call | solution.py:103
  118.0 3.0 %collective-permute-done.12 = bf16[512,1024]{1,0:T(8,128)(2,1)} collective-permute-done((bf16[512,1024]{1,0:T(8,128)(2,1)}, bf16[512,1024]{1,0:T(8,128)(2,1)}, u32[]{:S(2)}, u32[]{:S(2)}) %collective-permute-start.12) | collective-permute-done | bytes 1048608 | tf_op jit(solution)/shard_map/ppermute | solution.py:229
  121.0 3.2 %fusion.7 = bf16[64,8,1024]{2,1,0:T(8,128)(2,1)} fusion(f32[512,1024]{1,0:T(8,128)} %shard_map.112, bf16[512,1024]{1,0:T(8,128)(2,1)} %collective-permute-done.12), kind=kLoop, calls=%fused_computation.17 | loop fusion | flops 1572864 | bytes 4194304 | tf_op jit(solution)/shard_map/reshape | solution.py:292
  124.2 10.5 %all-to-all-start.3 = ((bf16[64,8,1024]{2,1,0:T(8,128)(2,1)}), bf16[64,8,1024]{2,1,0:T(8,128)(2,1)}, u32[]{:S(2)}, u32[]{:S(2)}) async-start(bf16[64,8,1024]{2,1,0:T(8,128)(2,1)} %fusion.7), calls=%async_computation.3 | async-start | bytes 2097152 | tf_op jit(solution)/shard_map/all_to_all | solution.py:293
  136.0 4.0 %fusion.48 = f32[256,704]{0,1:T(8,128)} fusion(bf16[256,2048]{1,0:T(8,128)(2,1)} %copy-done.10, bf16[2048,704]{0,1:T(8,128)(2,1)} %param.19), kind=kOutput, calls=%fused_computation.86 | convolution fusion | flops 738197504 | bytes 4653056 | tf_op jit(solution)/shard_map/dot_general | solution.py:28
  140.0 8.0 %shard_map.111 = bf16[512,1024]{1,0:T(8,128)(2,1)} custom-call(f32[1,2048]{1,0:T(1,128)} %bitcast.68, bf16[512,1024]{1,0:T(8,128)(2,1)} %collective-permute-done.9.x_in, bf16[352,2048]{1,0:T(8,128)(2,1)} %bitcast.54, bf16[352,2048]{1,0:T(8,128)(2,1)} %collective-permute-done.6.gate_b, bf16[352,2048]{1,0:T(8,128)(2,1)} %bitcast.59, ...), custom_call_target="tpu_custom_call" | custom-call | flops 2214592512 | bytes 10747904 | tf_op jit(solution)/shard_map/pallas_call | solution.py:103
  149.6 7.0 %convolution_multiply_fusion.base = f32[256,2048]{1,0:T(8,128)} fusion(bf16[704,2048]{1,0:T(8,128)(2,1)S(1)} %copy-done, f32[256]{0:T(256)S(1)} %add_divide_fusion, f32[256,704]{0,1:T(8,128)} %fusion.48, bf16[256,2048]{1,0:T(8,128)(2,1)} %copy-done.10, bf16[2048,704]{0,1:T(8,128)(2,1)} %param.20), kind=kOutput, calls=%fused_computation | convolution fusion | flops 1478000640 | bytes 9634816 | tf_op jit(solution)/shard_map/dot_general | solution.py:28
  156.6 8.3 %shard_map.110 = f32[512,1024]{1,0:T(8,128)} custom-call(f32[1,2048]{1,0:T(1,128)} %bitcast.69, bf16[512,1024]{1,0:T(8,128)(2,1)} %bitcast.14.x_in, bf16[352,2048]{1,0:T(8,128)(2,1)} %bitcast.55, bf16[352,2048]{1,0:T(8,128)(2,1)} %collective-permute-done.6.gate_b, bf16[352,2048]{1,0:T(8,128)(2,1)} %bitcast.60, ...), custom_call_target="tpu_custom_call" | custom-call | flops 2214592512 | bytes 10747904 | tf_op jit(solution)/shard_map/pallas_call | solution.py:103
  164.9 3.2 %fusion.6 = bf16[64,8,1024]{2,1,0:T(8,128)(2,1)} fusion(f32[512,1024]{1,0:T(8,128)} %shard_map.110, bf16[512,1024]{1,0:T(8,128)(2,1)} %collective-permute-done.10), kind=kLoop, calls=%fused_computation.16 | loop fusion | flops 1572864 | bytes 4194304 | tf_op jit(solution)/shard_map/reshape | solution.py:292
  168.1 12.0 %all-to-all-start.1 = ((bf16[64,8,1024]{2,1,0:T(8,128)(2,1)}), bf16[64,8,1024]{2,1,0:T(8,128)(2,1)}, u32[]{:S(2)}, u32[]{:S(2)}) async-start(bf16[64,8,1024]{2,1,0:T(8,128)(2,1)} %fusion.6), calls=%async_computation.1 | async-start | bytes 2097152 | tf_op jit(solution)/shard_map/all_to_all | solution.py:293
  186.7 2.5 %shard_map.114.base = f32[256,2048]{1,0:T(8,128)S(1)} custom-call(bf16[2,256,512]{2,1,0:T(8,128)(2,1)S(1)} %get-tuple-element.20.mix_hi, bf16[2,256,512]{2,1,0:T(8,128)(2,1)S(1)} %get-tuple-element.21.mix_lo, bf16[512,1024]{1,0:T(8,128)(2,1)} %bitcast.27.rows, f32[256,2048]{1,0:T(8,128)S(1)} %copy-done.5), custom_call_target="tpu_custom_call" | custom-call | flops 1073741824 | bytes 4194304 | tf_op jit(solution)/shard_map/pallas_call | solution.py:161
  190.6 18.2 %all-to-all-done.1 = bf16[64,8,1024]{2,1,0:T(8,128)(2,1)} async-done(((bf16[64,8,1024]{2,1,0:T(8,128)(2,1)}), bf16[64,8,1024]{2,1,0:T(8,128)(2,1)}, u32[]{:S(2)}, u32[]{:S(2)}) %all-to-all-start.1) | async-done | bytes 1048608 | tf_op jit(solution)/shard_map/all_to_all | solution.py:293
  211.5 2.5 %shard_map.115 = (f32[256,512]{1,0:T(8,128)S(1)}, f32[256,512]{1,0:T(8,128)S(1)}, bf16[256,512]{1,0:T(8,128)(2,1)S(1)}, bf16[256,512]{1,0:T(8,128)(2,1)S(1)}) custom-call(s32[4]{0:T(128)S(1)} %add_multiply_fusion.starts, bf16[2,256,512]{2,1,0:T(8,128)(2,1)S(1)} %copy-done.6, bf16[2,256,512]{2,1,0:T(8,128)(2,1)S(1)} %get-tuple-element.18.mix_lo, ...), custom_call_target="tpu_custom_call" | custom-call | flops 1073741824 | bytes 4194304 | tf_op jit(solution)/shard_map/pallas_call | solution.py:185
  213.9 2.6 %collective-permute-start.14 = (bf16[256,512]{1,0:T(8,128)(2,1)S(1)}, bf16[256,512]{1,0:T(8,128)(2,1)S(1)}, u32[]{:S(2)}, u32[]{:S(2)}) collective-permute-start(bf16[256,512]{1,0:T(8,128)(2,1)S(1)} %get-tuple-element.26), channel_id=1, source_target_pairs={{0,3},{1,2},{2,1},{3,0},{4,5},{5,4},{6,7},{7,6},{8,11},{9,10},{10,... | collective-permute-start | bytes 786440 | tf_op jit(solution)/shard_map/ppermute | solution.py:229
  216.7 4.3 %collective-permute-done.14 = bf16[256,512]{1,0:T(8,128)(2,1)S(1)} collective-permute-done((bf16[256,512]{1,0:T(8,128)(2,1)S(1)}, bf16[256,512]{1,0:T(8,128)(2,1)S(1)}, u32[]{:S(2)}, u32[]{:S(2)}) %collective-permute-start.14) | collective-permute-done | bytes 262176 | tf_op jit(solution)/shard_map/ppermute | solution.py:229
  221.0 4.5 %collective-permute-start.15 = (bf16[256,512]{1,0:T(8,128)(2,1)S(1)}, bf16[256,512]{1,0:T(8,128)(2,1)S(1)}, u32[]{:S(2)}, u32[]{:S(2)}) collective-permute-start(bf16[256,512]{1,0:T(8,128)(2,1)S(1)} %add_convert_fusion.3), channel_id=1, source_target_pairs={{0,1},{1,0},{2,3},{3,2},{4,7},{5,6},{6,5},{7,4},{8,9},{9,8},{10,11... | collective-permute-start | bytes 786440 | tf_op jit(solution)/shard_map/ppermute | solution.py:226
  225.5 4.3 %collective-permute-done.15 = bf16[256,512]{1,0:T(8,128)(2,1)S(1)} collective-permute-done((bf16[256,512]{1,0:T(8,128)(2,1)S(1)}, bf16[256,512]{1,0:T(8,128)(2,1)S(1)}, u32[]{:S(2)}, u32[]{:S(2)}) %collective-permute-start.15) | collective-permute-done | bytes 262176 | tf_op jit(solution)/shard_map/ppermute | solution.py:226
  (89 shorter events, 39.5 us)
Async XLA Ops:
  0.0 149.6 %copy-start = (bf16[704,2048]{1,0:T(8,128)(2,1)S(1)}, bf16[704,2048]{1,0:T(8,128)(2,1)}, u32[]{:S(2)}) copy-start(bf16[704,2048]{1,0:T(8,128)(2,1)} %param.21) | copy-start | bytes 8650756
  0.0 9.3 %collective-permute-start = (bf16[256,512]{1,0:T(8,128)(2,1)}, bf16[256,512]{1,0:T(8,128)(2,1)S(1)}, u32[]{:S(2)}, u32[]{:S(2)}) collective-permute-start(bf16[256,512]{1,0:T(8,128)(2,1)} %part_0.1), channel_id=1, source_target_pairs={{0,1},{1,0},{2,3},{3,2},{4,7},{5,6},{6,5},{7,4},{8,9},{9,8},{10,11... | collective-permute-start | bytes 786440 | tf_op jit(solution)/shard_map/ppermute | solution.py:226
  2.2 8.1 %collective-permute-start.1 = (bf16[256,512]{1,0:T(8,128)(2,1)}, bf16[256,512]{1,0:T(8,128)(2,1)S(1)}, u32[]{:S(2)}, u32[]{:S(2)}) collective-permute-start(bf16[256,512]{1,0:T(8,128)(2,1)} %part_0.1), channel_id=1, source_target_pairs={{0,3},{1,2},{2,1},{3,0},{4,5},{5,4},{6,7},{7,6},{8,11},{9,10},{10,... | collective-permute-start | bytes 786440 | tf_op jit(solution)/shard_map/ppermute | solution.py:229
  9.3 6.4 %collective-permute-start.2 = (bf16[256,512]{1,0:T(8,128)(2,1)S(1)}, bf16[256,512]{1,0:T(8,128)(2,1)S(1)}, u32[]{:S(2)}, u32[]{:S(2)}) collective-permute-start(bf16[256,512]{1,0:T(8,128)(2,1)S(1)} %collective-permute-done.part_1), channel_id=1, source_target_pairs={{0,3},{1,2},{2,1},{3,0},{4,5},{5,4},{6,7},{7,6},{8,11},{9,10},{10,... | collective-permute-start | bytes 786440 | tf_op jit(solution)/shard_map/ppermute | solution.py:229
  10.1 26.3 %copy-start.13 = (bf16[512,60]{0,1:T(8,128)(2,1)S(1)}, bf16[512,60]{0,1:T(8,128)(2,1)}, u32[]{:S(2)}) copy-start(bf16[512,60]{0,1:T(8,128)(2,1)} %param.13) | copy-start | bytes 184324
  10.1 58.5 %copy-start.14 = (bf16[2048]{0:T(1024)(128)(2,1)S(1)}, bf16[2048]{0:T(1024)(128)(2,1)}, u32[]{:S(2)}) copy-start(bf16[2048]{0:T(1024)(128)(2,1)} %param.14) | copy-start | bytes 12292
  21.5 40.6 %all-to-all-start.2 = ((bf16[64,8,1024]{2,1,0:T(8,128)(2,1)}), bf16[64,8,1024]{2,1,0:T(8,128)(2,1)}, u32[]{:S(2)}, u32[]{:S(2)}) async-start(bf16[64,8,1024]{2,1,0:T(8,128)(2,1)} %bitcast.50), calls=%async_computation.2 | async-start | bytes 2097152 | tf_op jit(solution)/shard_map/all_to_all | solution.py:286
  33.4 63.6 %collective-permute-start.6 = (bf16[352,2048]{1,0:T(8,128)(2,1)}, bf16[352,2048]{1,0:T(8,128)(2,1)}, u32[]{:S(2)}, u32[]{:S(2)}) collective-permute-start(bf16[352,2048]{1,0:T(8,128)(2,1)} %bitcast.51), channel_id=1, source_target_pairs={{0,1},{1,0},{2,3},{3,2},{4,7},{5,6},{6,5},{7,4},{8,9},{9,8},{10,11... | collective-permute-start | bytes 4325384 | tf_op jit(solution)/shard_map/ppermute | solution.py:226
  34.3 63.3 %collective-permute-start.7 = (bf16[352,2048]{1,0:T(8,128)(2,1)}, bf16[352,2048]{1,0:T(8,128)(2,1)}, u32[]{:S(2)}, u32[]{:S(2)}) collective-permute-start(bf16[352,2048]{1,0:T(8,128)(2,1)} %bitcast.56), channel_id=1, source_target_pairs={{0,1},{1,0},{2,3},{3,2},{4,7},{5,6},{6,5},{7,4},{8,9},{9,8},{10,11... | collective-permute-start | bytes 4325384 | tf_op jit(solution)/shard_map/ppermute | solution.py:226
  35.5 62.2 %collective-permute-start.8 = (bf16[352,2048]{1,0:T(8,128)(2,1)}, bf16[352,2048]{1,0:T(8,128)(2,1)}, u32[]{:S(2)}, u32[]{:S(2)}) collective-permute-start(bf16[352,2048]{1,0:T(8,128)(2,1)} %bitcast.61), channel_id=1, source_target_pairs={{0,1},{1,0},{2,3},{3,2},{4,7},{5,6},{6,5},{7,4},{8,9},{9,8},{10,11... | collective-permute-start | bytes 4325384 | tf_op jit(solution)/shard_map/ppermute | solution.py:226
  36.4 59.3 %collective-permute-start.3 = (bf16[512,60]{0,1:T(8,128)(2,1)S(1)}, bf16[512,60]{0,1:T(8,128)(2,1)}, u32[]{:S(2)}, u32[]{:S(2)}) collective-permute-start(bf16[512,60]{0,1:T(8,128)(2,1)S(1)} %copy-done.13), channel_id=1, source_target_pairs={{0,1},{1,0},{2,3},{3,2},{4,7},{5,6},{6,5},{7,4},{8,9},{9,8},{10,11... | collective-permute-start | bytes 184328 | tf_op jit(solution)/shard_map/ppermute | solution.py:226
  62.1 35.6 %collective-permute-start.11 = (bf16[512,1024]{1,0:T(8,128)(2,1)}, bf16[512,1024]{1,0:T(8,128)(2,1)}, u32[]{:S(2)}, u32[]{:S(2)}) collective-permute-start(bf16[512,1024]{1,0:T(8,128)(2,1)} %bitcast.25.x_in), channel_id=1, source_target_pairs={{0,3},{1,2},{2,1},{3,0},{4,5},{5,4},{6,7},{7,6},{8,11},{9,10},{10,... | collective-permute-start | bytes 3145736 | tf_op jit(solution)/shard_map/ppermute | solution.py:229
  71.1 37.8 %all-to-all-start = ((bf16[64,8,1024]{2,1,0:T(8,128)(2,1)}), bf16[64,8,1024]{2,1,0:T(8,128)(2,1)}, u32[]{:S(2)}, u32[]{:S(2)}) async-start(bf16[64,8,1024]{2,1,0:T(8,128)(2,1)} %bitcast.49), calls=%async_computation | async-start | bytes 2097152 | tf_op jit(solution)/shard_map/all_to_all | solution.py:286
  95.6 85.7 %collective-permute-start.4 = (bf16[512,60]{0,1:T(8,128)(2,1)S(1)}, bf16[512,60]{0,1:T(8,128)(2,1)}, u32[]{:S(2)}, u32[]{:S(2)}) collective-permute-start(bf16[512,60]{0,1:T(8,128)(2,1)S(1)} %copy-done.13), channel_id=1, source_target_pairs={{0,3},{1,2},{2,1},{3,0},{4,5},{5,4},{6,7},{7,6},{8,11},{9,10},{10,... | collective-permute-start | bytes 184328 | tf_op jit(solution)/shard_map/ppermute | solution.py:229
  97.0 85.7 %collective-permute-start.5 = (bf16[512,60]{0,1:T(8,128)(2,1)}, bf16[512,60]{0,1:T(8,128)(2,1)}, u32[]{:S(2)}, u32[]{:S(2)}) collective-permute-start(bf16[512,60]{0,1:T(8,128)(2,1)} %collective-permute-done.3), channel_id=1, source_target_pairs={{0,3},{1,2},{2,1},{3,0},{4,5},{5,4},{6,7},{7,6},{8,11},{9,10},{10,... | collective-permute-start | bytes 184328 | tf_op jit(solution)/shard_map/ppermute | solution.py:229
  105.8 15.2 %collective-permute-start.12 = (bf16[512,1024]{1,0:T(8,128)(2,1)}, bf16[512,1024]{1,0:T(8,128)(2,1)}, u32[]{:S(2)}, u32[]{:S(2)}) collective-permute-start(bf16[512,1024]{1,0:T(8,128)(2,1)} %shard_map.113), channel_id=1, source_target_pairs={{0,3},{1,2},{2,1},{3,0},{4,5},{5,4},{6,7},{7,6},{8,11},{9,10},{10,... | collective-permute-start | bytes 3145736 | tf_op jit(solution)/shard_map/ppermute | solution.py:229
  108.9 31.0 %collective-permute-start.9 = (bf16[512,1024]{1,0:T(8,128)(2,1)}, bf16[512,1024]{1,0:T(8,128)(2,1)}, u32[]{:S(2)}, u32[]{:S(2)}) collective-permute-start(bf16[512,1024]{1,0:T(8,128)(2,1)} %bitcast.14.x_in), channel_id=1, source_target_pairs={{0,3},{1,2},{2,1},{3,0},{4,5},{5,4},{6,7},{7,6},{8,11},{9,10},{10,... | collective-permute-start | bytes 3145736 | tf_op jit(solution)/shard_map/ppermute | solution.py:229
  124.2 43.9 %all-to-all-start.3 = ((bf16[64,8,1024]{2,1,0:T(8,128)(2,1)}), bf16[64,8,1024]{2,1,0:T(8,128)(2,1)}, u32[]{:S(2)}, u32[]{:S(2)}) async-start(bf16[64,8,1024]{2,1,0:T(8,128)(2,1)} %fusion.7), calls=%async_computation.3 | async-start | bytes 2097152 | tf_op jit(solution)/shard_map/all_to_all | solution.py:293
  148.0 16.9 %collective-permute-start.10 = (bf16[512,1024]{1,0:T(8,128)(2,1)}, bf16[512,1024]{1,0:T(8,128)(2,1)}, u32[]{:S(2)}, u32[]{:S(2)}) collective-permute-start(bf16[512,1024]{1,0:T(8,128)(2,1)} %shard_map.111), channel_id=1, source_target_pairs={{0,3},{1,2},{2,1},{3,0},{4,5},{5,4},{6,7},{7,6},{8,11},{9,10},{10,... | collective-permute-start | bytes 3145736 | tf_op jit(solution)/shard_map/ppermute | solution.py:229
  168.1 16.4 %copy-start.11 = (pred[2,256,512]{2,1,0:T(8,128)(4,1)S(1)}, pred[2,256,512]{2,1,0:T(8,128)(4,1)}, u32[]{:S(2)}) copy-start(pred[2,256,512]{2,1,0:T(8,128)(4,1)} %broadcast_compare_fusion) | copy-start | bytes 786436
  168.1 40.7 %all-to-all-start.1 = ((bf16[64,8,1024]{2,1,0:T(8,128)(2,1)}), bf16[64,8,1024]{2,1,0:T(8,128)(2,1)}, u32[]{:S(2)}, u32[]{:S(2)}) async-start(bf16[64,8,1024]{2,1,0:T(8,128)(2,1)} %fusion.6), calls=%async_computation.1 | async-start | bytes 2097152 | tf_op jit(solution)/shard_map/all_to_all | solution.py:293
  213.9 7.0 %collective-permute-start.14 = (bf16[256,512]{1,0:T(8,128)(2,1)S(1)}, bf16[256,512]{1,0:T(8,128)(2,1)S(1)}, u32[]{:S(2)}, u32[]{:S(2)}) collective-permute-start(bf16[256,512]{1,0:T(8,128)(2,1)S(1)} %get-tuple-element.26), channel_id=1, source_target_pairs={{0,3},{1,2},{2,1},{3,0},{4,5},{5,4},{6,7},{7,6},{8,11},{9,10},{10,... | collective-permute-start | bytes 786440 | tf_op jit(solution)/shard_map/ppermute | solution.py:229
  216.6 8.9 %collective-permute-start.13 = (bf16[256,512]{1,0:T(8,128)(2,1)S(1)}, bf16[256,512]{1,0:T(8,128)(2,1)S(1)}, u32[]{:S(2)}, u32[]{:S(2)}) collective-permute-start(bf16[256,512]{1,0:T(8,128)(2,1)S(1)} %get-tuple-element.24), channel_id=1, source_target_pairs={{0,3},{1,2},{2,1},{3,0},{4,5},{5,4},{6,7},{7,6},{8,11},{9,10},{10,... | collective-permute-start | bytes 786440 | tf_op jit(solution)/shard_map/ppermute | solution.py:229
  221.0 8.8 %collective-permute-start.15 = (bf16[256,512]{1,0:T(8,128)(2,1)S(1)}, bf16[256,512]{1,0:T(8,128)(2,1)S(1)}, u32[]{:S(2)}, u32[]{:S(2)}) collective-permute-start(bf16[256,512]{1,0:T(8,128)(2,1)S(1)} %add_convert_fusion.3), channel_id=1, source_target_pairs={{0,1},{1,0},{2,3},{3,2},{4,7},{5,6},{6,5},{7,4},{8,9},{9,8},{10,11... | collective-permute-start | bytes 786440 | tf_op jit(solution)/shard_map/ppermute | solution.py:226
  (11 other events, 29.8 us)

commit v2 on v1

--- a/solution.py
+++ b/solution.py
@@ -32,7 +32,6 @@
 VMEM = pl.BlockSpec(memory_space=pltpu.VMEM)
 SMEM = pl.BlockSpec(memory_space=pltpu.SMEM)
 BIG = pltpu.CompilerParams(vmem_limit_bytes=60 * 1024 * 1024)
-SMALL = pltpu.CompilerParams(vmem_limit_bytes=24 * 1024 * 1024)
 
 
 def load(pairs, sems):
@@ -48,11 +47,11 @@
 
 
 def ffn_kernel(gain, x_in, gate_a, gate_b, up_a, up_b, down_a, down_b, out, xv, x, gate_w, up_w, down_w, y, sems):
-    pairs = [(x_in, xv), *halves((gate_a, gate_b), gate_w), *halves((up_a, up_b), up_w)]
-    copies = load(pairs + halves((down_a, down_b), down_w), sems)
     rows, full = x.shape
     half = full // 2
-    copies[0].wait()
+    load([(x_in, xv)], sems)[0].wait()
+    pairs = halves((gate_a, gate_b), gate_w) + halves((up_a, up_b), up_w) + halves((down_a, down_b), down_w)
+    copies = load(pairs, sems)
     small = 32
     first = lax.broadcasted_iota(jnp.int32, (small // 8, 8, half), 1) < 4
 
@@ -72,14 +71,14 @@
         return carry
 
     lax.fori_loop(0, rows // small, norm_step, 0)
-    for c in copies[1:3]:
+    for c in copies[:2]:
         c.wait()
     gate = dot(x[...], gate_w[...], ((1,), (1,)))
-    for c in copies[3:5]:
+    for c in copies[2:4]:
         c.wait()
     up = dot(x[...], up_w[...], ((1,), (1,)))
     hidden = (gate / (1.0 + jnp.exp(-gate)) * up).astype(BF16)
-    for c in copies[5:]:
+    for c in copies[4:]:
         c.wait()
     y[...] = dot(hidden, down_w[...])
 
@@ -110,7 +109,7 @@
             pltpu.VMEM((rows, full), BF16),
             *[pltpu.VMEM((units, full), BF16)] * 3,
             pltpu.VMEM((rows, full), F32),
-            pltpu.SemaphoreType.DMA((7,)),
+            pltpu.SemaphoreType.DMA((6,)),
         ],
         cost_estimate=pl.CostEstimate(
             flops=6 * rows * full * units,
@@ -121,33 +120,51 @@
     )(gain, x, *weights)
 
 
-def dispatch_kernel(starts, pick, part_0, part_1, part_2, part_3, whole, *outs):
+def dispatch_kernel(starts, pick, part_0, part_1, part_2, part_3, out, *whole):
     width = part_0.shape[1]
-    rows, half = outs[0].shape
-    for k, part in enumerate((part_0, part_1, part_2, part_3)):
-        whole[:, pl.ds(pl.multiple_of(starts[k], width), width)] = part[...]
+    rows, half = out.shape
     upper_row = lax.broadcasted_iota(jnp.int32, (rows, width), 0) % 8 // 4
     for k, a, b in ((0, part_0, part_3), (1, part_1, part_2)):
         is_a = upper_row == starts[k] // half
         at = pl.ds(pl.multiple_of(starts[k] % half, width), width)
-        for c, out in enumerate(outs):
-            out[:, at] = jnp.where(is_a, dot(pick[c], a[...]), dot(pick[c], b[...])).astype(BF16)
-
-
-def dispatched_rows(starts, pick, parts):
+        out[:, at] = jnp.where(is_a, dot(pick[...], a[...]), dot(pick[...], b[...])).astype(BF16)
+    for w in whole:
+        for k, part in enumerate((part_0, part_1, part_2, part_3)):
+            w[:, pl.ds(pl.multiple_of(starts[k], width), width)] = part[...]
+
+
+def dispatched_rows(starts, pick, parts, with_tokens):
     tokens, width = parts[0].shape
-    full, rows = width * len(parts), pick.shape[1]
-    out = jax.ShapeDtypeStruct((rows, full // 2), BF16)
+    full, rows = width * len(parts), pick.shape[0]
+    shapes = [(rows, full // 2)] + [(tokens, full)] * with_tokens
     return pl.pallas_call(
         dispatch_kernel,
-        out_shape=[jax.ShapeDtypeStruct((tokens, full), BF16)] + [out] * CHUNKS,
+        out_shape=[jax.ShapeDtypeStruct(shape, BF16) for shape in shapes],
         in_specs=[SMEM] + [VMEM] * 5,
-        out_specs=[VMEM] * (1 + CHUNKS),
+        out_specs=[VMEM] * len(shapes),
         cost_estimate=pl.CostEstimate(
-            flops=2 * pick.size * full, transcendentals=0, bytes_accessed=8 * tokens * full
-        ),
-        compiler_params=SMALL,
+            flops=2 * pick.size * full, transcendentals=0, bytes_accessed=4 * tokens * full
+        ),
+        compiler_params=BIG,
     )(starts, pick, *parts)
+
+
+def join_kernel(kept, got, out):
+    out[...] = (kept[...] + got[...].astype(F32)).astype(BF16)
+
+
+def joined(kept, got):
+    rows, half = kept.shape
+    block = pl.BlockSpec((rows // 4, half), lambda i: (i, 0))
+    return pl.pallas_call(
+        join_kernel,
+        out_shape=jax.ShapeDtypeStruct(kept.shape, BF16),
+        grid=(4,),
+        in_specs=[block] * 2,
+        out_specs=block,
+        cost_estimate=pl.CostEstimate(flops=kept.size, transcendentals=0, bytes_accessed=8 * kept.size),
+        compiler_params=BIG,
+    )(kept, got)
 
 
 def gather_kernel(mix_hi, mix_lo, rows, base, out):
@@ -166,13 +183,13 @@
         cost_estimate=pl.CostEstimate(
             flops=4 * mix_hi.size * rows.shape[1], transcendentals=0, bytes_accessed=8 * base.size
         ),
-        compiler_params=SMALL,
+        compiler_params=BIG,
     )(mix_hi, mix_lo, rows, base)
 
 
-def combine_kernel(starts, mix_hi, mix_lo, rows, base, mine, near, across, diag):
-    width, half = mine.shape[1], rows.shape[1]
-    for k, out in ((3, diag), (2, across), (1, near), (0, mine)):
+def combine_kernel(starts, mix_hi, mix_lo, rows, base, *outs):
+    width, half = outs[0].shape[1], rows.shape[1]
+    for k, out in enumerate(outs):
         h = starts[k] // half
         from_rows = pl.ds(pl.multiple_of(starts[k] % half, width), width)
         value = dot(mix_hi[h], rows[:, from_rows]) + dot(mix_lo[h], rows[:, from_rows])
@@ -180,17 +197,18 @@
         out[...] = (base[:, at] + value).astype(out.dtype)
 
 
-def combined(starts, mix_hi, mix_lo, rows, base):
+def combined(starts, mix_hi, mix_lo, rows, base, dtype):
     tokens, full = base.shape
+    count = starts.shape[0]
     return pl.pallas_call(
         combine_kernel,
-        out_shape=[jax.ShapeDtypeStruct((tokens, full // 4), d) for d in (F32, F32, BF16, BF16)],
+        out_shape=[jax.ShapeDtypeStruct((tokens, full // 4), dtype)] * count,
         in_specs=[SMEM] + [VMEM] * 4,
-        out_specs=[VMEM] * 4,
+        out_specs=[VMEM] * count,
         cost_estimate=pl.CostEstimate(
-            flops=4 * mix_hi.size * full // 2, transcendentals=0, bytes_accessed=8 * tokens * full
-        ),
-        compiler_params=SMALL,
+            flops=mix_hi.size * full, transcendentals=0, bytes_accessed=8 * tokens * full
+        ),
+        compiler_params=BIG,
     )(starts, mix_hi, mix_lo, rows, base)
 
 
@@ -251,7 +269,9 @@
         hit = dot(key, spread)[None] == mine[:, None, :]
         pick = (dot(spread, key, ((0,), (1,)))[None] == mine[:, :, None]).astype(BF16)
 
-        whole, *outgoing = dispatched_rows(starts, pick, parts)
+        (outgoing_0,) = dispatched_rows(starts, pick[0], parts, False)
+        outgoing_1, whole = dispatched_rows(starts, pick[1], parts, True)
+        outgoing = (outgoing_0, outgoing_1)
 
         values = whole.astype(F32)
         inv_rms = lax.rsqrt(jnp.mean(values * values, axis=-1, keepdims=True) + 1e-06)
@@ -289,13 +309,14 @@
             sent = half_ffn(gain, arrived_far, weights, BF16)
             got = to_across(sent)
             kept = half_ffn(gain, arrived, weights, F32)
-            out = (kept + got.astype(F32)).astype(BF16).reshape(there.shape)
+            out = joined(kept, got).reshape(there.shape)
             returned = lax.all_to_all(out, "ep", 0, 0, tiled=True)
             returned = returned.reshape(outgoing[c].shape)
             if c < CHUNKS - 1:
                 acc = gathered(*mixes[c], returned, acc)
             else:
-                total_me, total_near, for_across, for_diag = combined(starts, *mixes[c], returned, acc)
+                for_diag, for_across = combined(starts[:1:-1], *mixes[c], returned, acc, BF16)
+                total_near, total_me = combined(starts[1::-1], *mixes[c], returned, acc, F32)
         came_near = to_across(for_diag)
         came_me = to_across(for_across)
         again = to_near((total_near + came_near.astype(F32)).astype(BF16))

time: 233 us -> 272 us (1.17)
  waiting for transfers between devices: 81 us -> 105 us
  Pallas kernels: 39.6 us -> 61.1 us
  local copies, waits for them, and re-layouts: 11.3 us -> 4.95 us
  other arithmetic: 11.6 us -> 8.75 us
    ppermute x6, waiting for transfers between devices: 25.6 us -> 55.8 us  [to_near(): return lax.ppermute(value, BOTH, near_pairs)]
    pallas_call x1 -> x4, Pallas kernels: 1.88 us -> 13.9 us  [the longest x2 7.58 us: joined(): pl.pallas_call(join_kernel, out_shape=jax.ShapeDtypeStruct(kept.shape, BF...]
    unnamed x31 -> x17, local copies, waits for them, and re-layouts: 9.62 us -> 0.75 us
    ppermute x10, waiting for transfers between devices: 12.7 us -> 5.88 us  [to_across(): return lax.ppermute(value, BOTH, across_pairs)]
    reshape x2 -> x0, other arithmetic: 6.41 us -> none  [body(): out = (kept + got.astype(F32)).astype(BF16).reshape(there.shape)]
    pallas_call x1 -> x2, Pallas kernels: 2.49 us -> 7.44 us  [combined(): pl.pallas_call(combine_kernel, out_shape=[jax.ShapeDtypeStruct((tokens, f...]
  transfers between devices with their start and end apart: 20 -> 20, of which waited for: 8 -> 8; matrix products, arithmetic and copies ran while one was open for 13% -> 11% of each run, Pallas kernels for 15% -> 20%
where the time goes in v2:
time: 272 us; the launch traced here: 269 us
  waiting for transfers between devices  105 us (39%)
  starting transfers between devices  62.3 us (23%)
  Pallas kernels  61.1 us (22%)
  matrix products  18.7 us (7%)
  other arithmetic  8.75 us (3%)
  between operations  8.06 us (3%)
  local copies, waits for them, and re-layouts  4.95 us (2%)
    ppermute x6, waiting for transfers between devices, to_near(): return lax.ppermute(value, BOTH, near_pairs)  55.8 us
    pallas_call x4, Pallas kernels, half_ffn(): pl.pallas_call(ffn_kernel, out_shape=jax.ShapeDtypeStruct(x.shape, dtype)...  35 us
    all_to_all x2, waiting for transfers between devices, body(): arrived = lax.all_to_all(there, 'ep', 0, 0, tiled=True)  25.3 us
    all_to_all x2, starting transfers between devices, body(): returned = lax.all_to_all(out, 'ep', 0, 0, tiled=True)  22.4 us
    dot_general x12, matrix products, dot(): return lax.dot_general(a, b, (dims, ((), ())), preferred_element_type=F32)  18.7 us
    all_to_all x2, starting transfers between devices, body(): arrived = lax.all_to_all(there, 'ep', 0, 0, tiled=True)  17.8 us
    all_to_all x2, waiting for transfers between devices, body(): returned = lax.all_to_all(out, 'ep', 0, 0, tiled=True)  17.7 us
    ppermute x10, starting transfers between devices, to_across(): return lax.ppermute(value, BOTH, across_pairs)  11.3 us
  transfers between devices with their start and end apart: 20, of which 8 were waited for; matrix products, arithmetic and copies ran while one was open for 11% of the time, Pallas kernels for 20%

profile of v2, /device:TPU:8, one launch (start us, length us, event | category | flops | bytes accessed | tf_op | source)
XLA Modules:
  0.0 268.6 jit_solution(1828377006580951926)
XLA Ops:
  4.4 5.1 %collective-permute-done.part_1 = bf16[256,512]{1,0:T(8,128)(2,1)} collective-permute-done((bf16[256,512]{1,0:T(8,128)(2,1)}, bf16[256,512]{1,0:T(8,128)(2,1)}, u32[]{:S(2)}, u32[]{:S(2)}) %collective-permute-start) | collective-permute-done | bytes 262176 | tf_op jit(solution)/shard_map/ppermute | solution.py:244
  11.5 4.5 %collective-permute-done.2.part_3 = bf16[256,512]{1,0:T(8,128)(2,1)S(1)} collective-permute-done((bf16[256,512]{1,0:T(8,128)(2,1)}, bf16[256,512]{1,0:T(8,128)(2,1)S(1)}, u32[]{:S(2)}, u32[]{:S(2)}) %collective-permute-start.2) | collective-permute-done | bytes 262176 | tf_op jit(solution)/shard_map/ppermute | solution.py:247
  16.7 2.9 %shard_map.113 = bf16[512,1024]{1,0:T(8,128)(2,1)} custom-call(s32[4]{0:T(128)} %add_multiply_fusion.starts, bf16[512,256]{1,0:T(8,128)(2,1)} %get-tuple-element.29.pick, bf16[256,512]{1,0:T(8,128)(2,1)} %part_0.3, bf16[256,512]{1,0:T(8,128)(2,1)} %collective-permute-done.part_1, bf16[256,512]{1,0:T(8,128)(2,1)} %collective-permute-done.1.part_2, ...), custom_call_target="tpu_custom_call" | custom-call | flops 536870912 | bytes 2097152 | tf_op jit(solution)/shard_map/pallas_call | solution.py:140
  19.7 11.9 %all-to-all-start.2 = ((bf16[64,8,1024]{2,1,0:T(8,128)(2,1)}), bf16[64,8,1024]{2,1,0:T(8,128)(2,1)}, u32[]{:S(2)}, u32[]{:S(2)}) async-start(bf16[64,8,1024]{2,1,0:T(8,128)(2,1)} %bitcast.66), calls=%async_computation.2 | async-start | bytes 2097152 | tf_op jit(solution)/shard_map/all_to_all | solution.py:306
  31.6 3.4 %shard_map.109 = (bf16[512,1024]{1,0:T(8,128)(2,1)}, bf16[256,2048]{1,0:T(8,128)(2,1)}) custom-call(s32[4]{0:T(128)} %add_multiply_fusion.starts, bf16[512,256]{1,0:T(8,128)(2,1)} %get-tuple-element.30.pick, bf16[256,512]{1,0:T(8,128)(2,1)} %part_0.3, bf16[256,512]{1,0:T(8,128)(2,1)} %collective-permute-done.part_1, ...), custom_call_target="tpu_custom_call" | custom-call | flops 536870912 | bytes 2097152 | tf_op jit(solution)/shard_map/pallas_call | solution.py:140
  35.0 25.3 %all-to-all-done.2 = bf16[64,8,1024]{2,1,0:T(8,128)(2,1)} async-done(((bf16[64,8,1024]{2,1,0:T(8,128)(2,1)}), bf16[64,8,1024]{2,1,0:T(8,128)(2,1)}, u32[]{:S(2)}, u32[]{:S(2)}) %all-to-all-start.2) | async-done | bytes 1048608 | tf_op jit(solution)/shard_map/all_to_all | solution.py:306
  60.3 5.8 %all-to-all-start = ((bf16[64,8,1024]{2,1,0:T(8,128)(2,1)}), bf16[64,8,1024]{2,1,0:T(8,128)(2,1)}, u32[]{:S(2)}, u32[]{:S(2)}) async-start(bf16[64,8,1024]{2,1,0:T(8,128)(2,1)} %bitcast.69), calls=%async_computation | async-start | bytes 2097152 | tf_op jit(solution)/shard_map/all_to_all | solution.py:306
  82.0 46.4 %collective-permute-done.3 = bf16[512,60]{0,1:T(8,128)(2,1)} collective-permute-done((bf16[512,60]{0,1:T(8,128)(2,1)S(1)}, bf16[512,60]{0,1:T(8,128)(2,1)}, u32[]{:S(2)}, u32[]{:S(2)}) %collective-permute-start.3) | collective-permute-done | bytes 61472 | tf_op jit(solution)/shard_map/ppermute | solution.py:244
  130.5 8.7 %shard_map.115 = bf16[512,1024]{1,0:T(8,128)(2,1)} custom-call(f32[1,2048]{1,0:T(1,128)} %bitcast.70, bf16[512,1024]{1,0:T(8,128)(2,1)} %collective-permute-done.11.x_in, bf16[352,2048]{1,0:T(8,128)(2,1)} %bitcast.52, bf16[352,2048]{1,0:T(8,128)(2,1)} %collective-permute-done.6.gate_b, bf16[352,2048]{1,0:T(8,128)(2,1)} %bitcast.57, ...), custom_call_target="tpu_custom_call" | custom-call | flops 2214592512 | bytes 10747904 | tf_op jit(solution)/shard_map/pallas_call | solution.py:102
  144.2 8.9 %shard_map.114.kept = f32[512,1024]{1,0:T(8,128)} custom-call(f32[1,2048]{1,0:T(1,128)} %bitcast.71, bf16[512,1024]{1,0:T(8,128)(2,1)} %bitcast.27.x_in, bf16[352,2048]{1,0:T(8,128)(2,1)} %bitcast.53, bf16[352,2048]{1,0:T(8,128)(2,1)} %collective-permute-done.6.gate_b, bf16[352,2048]{1,0:T(8,128)(2,1)} %bitcast.58, ...), custom_call_target="tpu_custom_call" | custom-call | flops 2214592512 | bytes 10747904 | tf_op jit(solution)/shard_map/pallas_call | solution.py:102
  154.3 3.8 %shard_map.116 = bf16[512,1024]{1,0:T(8,128)(2,1)} custom-call(f32[512,1024]{1,0:T(8,128)} %shard_map.114.kept, bf16[512,1024]{1,0:T(8,128)(2,1)} %collective-permute-done.12.got), custom_call_target="tpu_custom_call" | custom-call | flops 524288 | bytes 4194304 | tf_op jit(solution)/shard_map/pallas_call | solution.py:159
  158.1 10.5 %all-to-all-start.3 = ((bf16[64,8,1024]{2,1,0:T(8,128)(2,1)}), bf16[64,8,1024]{2,1,0:T(8,128)(2,1)}, u32[]{:S(2)}, u32[]{:S(2)}) async-start(bf16[64,8,1024]{2,1,0:T(8,128)(2,1)} %bitcast.68), calls=%async_computation.3 | async-start | bytes 2097152 | tf_op jit(solution)/shard_map/all_to_all | solution.py:313
  171.5 4.0 %fusion.47 = f32[256,704]{0,1:T(8,128)} fusion(bf16[256,2048]{1,0:T(8,128)(2,1)} %fusion.2, bf16[2048,704]{0,1:T(8,128)(2,1)} %param.19), kind=kOutput, calls=%fused_computation.85 | convolution fusion | flops 738197504 | bytes 4653056 | tf_op jit(solution)/shard_map/dot_general | solution.py:28
  175.5 8.6 %shard_map.111 = bf16[512,1024]{1,0:T(8,128)(2,1)} custom-call(f32[1,2048]{1,0:T(1,128)} %bitcast.72, bf16[512,1024]{1,0:T(8,128)(2,1)} %collective-permute-done.9.x_in, bf16[352,2048]{1,0:T(8,128)(2,1)} %bitcast.54, bf16[352,2048]{1,0:T(8,128)(2,1)} %collective-permute-done.6.gate_b, bf16[352,2048]{1,0:T(8,128)(2,1)} %bitcast.59, ...), custom_call_target="tpu_custom_call" | custom-call | flops 2214592512 | bytes 10747904 | tf_op jit(solution)/shard_map/pallas_call | solution.py:102
  185.7 6.9 %convolution_multiply_fusion.base = f32[256,2048]{1,0:T(8,128)} fusion(bf16[704,2048]{1,0:T(8,128)(2,1)S(1)} %copy-done, f32[256]{0:T(256)S(1)} %add_divide_fusion, f32[256,704]{0,1:T(8,128)} %fusion.47, bf16[256,2048]{1,0:T(8,128)(2,1)} %fusion.2, bf16[2048,704]{0,1:T(8,128)(2,1)} %param.20), kind=kOutput, calls=%fused_computation | convolution fusion | flops 1478000640 | bytes 9634816 | tf_op jit(solution)/shard_map/dot_general | solution.py:28
  192.6 8.9 %shard_map.110.kept = f32[512,1024]{1,0:T(8,128)} custom-call(f32[1,2048]{1,0:T(1,128)} %bitcast.73, bf16[512,1024]{1,0:T(8,128)(2,1)} %bitcast.15.x_in, bf16[352,2048]{1,0:T(8,128)(2,1)} %bitcast.55, bf16[352,2048]{1,0:T(8,128)(2,1)} %collective-permute-done.6.gate_b, bf16[352,2048]{1,0:T(8,128)(2,1)} %bitcast.60, ...), custom_call_target="tpu_custom_call" | custom-call | flops 2214592512 | bytes 10747904 | tf_op jit(solution)/shard_map/pallas_call | solution.py:102
  201.5 3.8 %shard_map.112 = bf16[512,1024]{1,0:T(8,128)(2,1)} custom-call(f32[512,1024]{1,0:T(8,128)} %shard_map.110.kept, bf16[512,1024]{1,0:T(8,128)(2,1)} %collective-permute-done.10.got), custom_call_target="tpu_custom_call" | custom-call | flops 524288 | bytes 4194304 | tf_op jit(solution)/shard_map/pallas_call | solution.py:159
  205.3 11.9 %all-to-all-start.1 = ((bf16[64,8,1024]{2,1,0:T(8,128)(2,1)}), bf16[64,8,1024]{2,1,0:T(8,128)(2,1)}, u32[]{:S(2)}, u32[]{:S(2)}) async-start(bf16[64,8,1024]{2,1,0:T(8,128)(2,1)} %bitcast.67), calls=%async_computation.1 | async-start | bytes 2097152 | tf_op jit(solution)/shard_map/all_to_all | solution.py:313
  223.4 4.8 %shard_map.117.base = f32[256,2048]{1,0:T(8,128)} custom-call(bf16[2,256,512]{2,1,0:T(8,128)(2,1)} %get-tuple-element.19.mix_hi, bf16[2,256,512]{2,1,0:T(8,128)(2,1)} %get-tuple-element.20.mix_lo, bf16[512,1024]{1,0:T(8,128)(2,1)} %bitcast.29.rows, f32[256,2048]{1,0:T(8,128)} %convolution_multiply_fusion.base), custom_call_target="tpu_custom_call" | custom-call | flops 1073741824 | bytes 4194304 | tf_op jit(solution)/shard_map/pallas_call | solution.py:178
  228.2 17.7 %all-to-all-done.1 = bf16[64,8,1024]{2,1,0:T(8,128)(2,1)} async-done(((bf16[64,8,1024]{2,1,0:T(8,128)(2,1)}), bf16[64,8,1024]{2,1,0:T(8,128)(2,1)}, u32[]{:S(2)}, u32[]{:S(2)}) %all-to-all-start.1) | async-done | bytes 1048608 | tf_op jit(solution)/shard_map/all_to_all | solution.py:313
  245.9 3.7 %shard_map.119 = (bf16[256,512]{1,0:T(8,128)(2,1)}, bf16[256,512]{1,0:T(8,128)(2,1)}) custom-call(s32[2]{0:T(128)} %rev.7.starts, bf16[2,256,512]{2,1,0:T(8,128)(2,1)} %get-tuple-element.16.mix_hi, bf16[2,256,512]{2,1,0:T(8,128)(2,1)} %get-tuple-element.17.mix_lo, bf16[512,1024]{1,0:T(8,128)(2,1)} %bitcast.24.rows, f32[256,2048]{1,0:T(8,128)} %shard_map.117.base), custom_call_target="tpu_custom_call" | custom-call | flops 536870912 | bytes 4194304 | tf_op jit(solution)/shard_map/pallas_call | solution.py:203
  252.9 3.8 %shard_map.118 = (f32[256,512]{1,0:T(8,128)}, f32[256,512]{1,0:T(8,128)}) custom-call(s32[2]{0:T(128)} %rev.6.starts, bf16[2,256,512]{2,1,0:T(8,128)(2,1)} %get-tuple-element.16.mix_hi, bf16[2,256,512]{2,1,0:T(8,128)(2,1)} %get-tuple-element.17.mix_lo, bf16[512,1024]{1,0:T(8,128)(2,1)} %bitcast.24.rows, f32[256,2048]{1,0:T(8,128)} %shard_map.117.base), custom_call_target="tpu_custom_call" | custom-call | flops 536870912 | bytes 4194304 | tf_op jit(solution)/shard_map/pallas_call | solution.py:203
  257.9 4.5 %collective-permute-start.15 = (bf16[256,512]{1,0:T(8,128)(2,1)S(1)}, bf16[256,512]{1,0:T(8,128)(2,1)S(1)}, u32[]{:S(2)}, u32[]{:S(2)}) collective-permute-start(bf16[256,512]{1,0:T(8,128)(2,1)S(1)} %add_convert_fusion.1), channel_id=1, source_target_pairs={{0,1},{1,0},{2,3},{3,2},{4,7},{5,6},{6,5},{7,4},{8,9},{9,8},{10,11... | collective-permute-start | bytes 786440 | tf_op jit(solution)/shard_map/ppermute | solution.py:244
  262.4 4.3 %collective-permute-done.15 = bf16[256,512]{1,0:T(8,128)(2,1)S(1)} collective-permute-done((bf16[256,512]{1,0:T(8,128)(2,1)S(1)}, bf16[256,512]{1,0:T(8,128)(2,1)S(1)}, u32[]{:S(2)}, u32[]{:S(2)}) %collective-permute-start.15) | collective-permute-done | bytes 262176 | tf_op jit(solution)/shard_map/ppermute | solution.py:244
  (81 shorter events, 40.6 us)
Async XLA Ops:
  0.0 185.7 %copy-start = (bf16[704,2048]{1,0:T(8,128)(2,1)S(1)}, bf16[704,2048]{1,0:T(8,128)(2,1)}, u32[]{:S(2)}) copy-start(bf16[704,2048]{1,0:T(8,128)(2,1)} %param.21) | copy-start | bytes 8650756
  0.0 9.4 %collective-permute-start = (bf16[256,512]{1,0:T(8,128)(2,1)}, bf16[256,512]{1,0:T(8,128)(2,1)}, u32[]{:S(2)}, u32[]{:S(2)}) collective-permute-start(bf16[256,512]{1,0:T(8,128)(2,1)} %part_0.3), channel_id=1, source_target_pairs={{0,1},{1,0},{2,3},{3,2},{4,7},{5,6},{6,5},{7,4},{8,9},{9,8},{10,11... | collective-permute-start | bytes 786440 | tf_op jit(solution)/shard_map/ppermute | solution.py:244
  2.2 9.4 %collective-permute-start.1 = (bf16[256,512]{1,0:T(8,128)(2,1)}, bf16[256,512]{1,0:T(8,128)(2,1)}, u32[]{:S(2)}, u32[]{:S(2)}) collective-permute-start(bf16[256,512]{1,0:T(8,128)(2,1)} %part_0.3), channel_id=1, source_target_pairs={{0,3},{1,2},{2,1},{3,0},{4,5},{5,4},{6,7},{7,6},{8,11},{9,10},{10,... | collective-permute-start | bytes 786440 | tf_op jit(solution)/shard_map/ppermute | solution.py:247
  9.4 6.6 %collective-permute-start.2 = (bf16[256,512]{1,0:T(8,128)(2,1)}, bf16[256,512]{1,0:T(8,128)(2,1)S(1)}, u32[]{:S(2)}, u32[]{:S(2)}) collective-permute-start(bf16[256,512]{1,0:T(8,128)(2,1)} %collective-permute-done.part_1), channel_id=1, source_target_pairs={{0,3},{1,2},{2,1},{3,0},{4,5},{5,4},{6,7},{7,6},{8,11},{9,10},{10,... | collective-permute-start | bytes 786440 | tf_op jit(solution)/shard_map/ppermute | solution.py:247
  19.7 40.6 %all-to-all-start.2 = ((bf16[64,8,1024]{2,1,0:T(8,128)(2,1)}), bf16[64,8,1024]{2,1,0:T(8,128)(2,1)}, u32[]{:S(2)}, u32[]{:S(2)}) async-start(bf16[64,8,1024]{2,1,0:T(8,128)(2,1)} %bitcast.66), calls=%async_computation.2 | async-start | bytes 2097152 | tf_op jit(solution)/shard_map/all_to_all | solution.py:306
  31.6 37.4 %copy-start.5 = (bf16[512,60]{0,1:T(8,128)(2,1)S(1)}, bf16[512,60]{0,1:T(8,128)(2,1)}, u32[]{:S(2)}) copy-start(bf16[512,60]{0,1:T(8,128)(2,1)} %param.13) | copy-start | bytes 184324
  31.6 40.1 %copy-start.6 = (s32[4]{0:T(128)S(1)}, s32[4]{0:T(128)}, u32[]{:S(2)}) copy-start(s32[4]{0:T(128)} %add_multiply_fusion.starts) | copy-start | bytes 52
  35.0 43.8 %copy-start.7 = (bf16[2048]{0:T(1024)(128)(2,1)S(1)}, bf16[2048]{0:T(1024)(128)(2,1)}, u32[]{:S(2)}) copy-start(bf16[2048]{0:T(1024)(128)(2,1)} %param.14) | copy-start | bytes 12292
  60.3 80.6 %all-to-all-start = ((bf16[64,8,1024]{2,1,0:T(8,128)(2,1)}), bf16[64,8,1024]{2,1,0:T(8,128)(2,1)}, u32[]{:S(2)}, u32[]{:S(2)}) async-start(bf16[64,8,1024]{2,1,0:T(8,128)(2,1)} %bitcast.69), calls=%async_computation | async-start | bytes 2097152 | tf_op jit(solution)/shard_map/all_to_all | solution.py:306
  66.2 63.6 %collective-permute-start.6 = (bf16[352,2048]{1,0:T(8,128)(2,1)}, bf16[352,2048]{1,0:T(8,128)(2,1)}, u32[]{:S(2)}, u32[]{:S(2)}) collective-permute-start(bf16[352,2048]{1,0:T(8,128)(2,1)} %bitcast.51), channel_id=1, source_target_pairs={{0,1},{1,0},{2,3},{3,2},{4,7},{5,6},{6,5},{7,4},{8,9},{9,8},{10,11... | collective-permute-start | bytes 4325384 | tf_op jit(solution)/shard_map/ppermute | solution.py:244
  67.0 63.4 %collective-permute-start.7 = (bf16[352,2048]{1,0:T(8,128)(2,1)}, bf16[352,2048]{1,0:T(8,128)(2,1)}, u32[]{:S(2)}, u32[]{:S(2)}) collective-permute-start(bf16[352,2048]{1,0:T(8,128)(2,1)} %bitcast.56), channel_id=1, source_target_pairs={{0,1},{1,0},{2,3},{3,2},{4,7},{5,6},{6,5},{7,4},{8,9},{9,8},{10,11... | collective-permute-start | bytes 4325384 | tf_op jit(solution)/shard_map/ppermute | solution.py:244
  68.3 62.2 %collective-permute-start.8 = (bf16[352,2048]{1,0:T(8,128)(2,1)}, bf16[352,2048]{1,0:T(8,128)(2,1)}, u32[]{:S(2)}, u32[]{:S(2)}) collective-permute-start(bf16[352,2048]{1,0:T(8,128)(2,1)} %bitcast.61), channel_id=1, source_target_pairs={{0,1},{1,0},{2,3},{3,2},{4,7},{5,6},{6,5},{7,4},{8,9},{9,8},{10,11... | collective-permute-start | bytes 4325384 | tf_op jit(solution)/shard_map/ppermute | solution.py:244
  69.0 59.4 %collective-permute-start.3 = (bf16[512,60]{0,1:T(8,128)(2,1)S(1)}, bf16[512,60]{0,1:T(8,128)(2,1)}, u32[]{:S(2)}, u32[]{:S(2)}) collective-permute-start(bf16[512,60]{0,1:T(8,128)(2,1)S(1)} %copy-done.5), channel_id=1, source_target_pairs={{0,1},{1,0},{2,3},{3,2},{4,7},{5,6},{6,5},{7,4},{8,9},{9,8},{10,11... | collective-permute-start | bytes 184328 | tf_op jit(solution)/shard_map/ppermute | solution.py:244
  70.3 60.1 %collective-permute-start.11 = (bf16[512,1024]{1,0:T(8,128)(2,1)}, bf16[512,1024]{1,0:T(8,128)(2,1)}, u32[]{:S(2)}, u32[]{:S(2)}) collective-permute-start(bf16[512,1024]{1,0:T(8,128)(2,1)} %bitcast.27.x_in), channel_id=1, source_target_pairs={{0,3},{1,2},{2,1},{3,0},{4,5},{5,4},{6,7},{7,6},{8,11},{9,10},{10,... | collective-permute-start | bytes 3145736 | tf_op jit(solution)/shard_map/ppermute | solution.py:247
  128.4 90.1 %collective-permute-start.4 = (bf16[512,60]{0,1:T(8,128)(2,1)S(1)}, bf16[512,60]{0,1:T(8,128)(2,1)}, u32[]{:S(2)}, u32[]{:S(2)}) collective-permute-start(bf16[512,60]{0,1:T(8,128)(2,1)S(1)} %copy-done.5), channel_id=1, source_target_pairs={{0,3},{1,2},{2,1},{3,0},{4,5},{5,4},{6,7},{7,6},{8,11},{9,10},{10,... | collective-permute-start | bytes 184328 | tf_op jit(solution)/shard_map/ppermute | solution.py:247
  129.8 90.0 %collective-permute-start.5 = (bf16[512,60]{0,1:T(8,128)(2,1)}, bf16[512,60]{0,1:T(8,128)(2,1)S(1)}, u32[]{:S(2)}, u32[]{:S(2)}) collective-permute-start(bf16[512,60]{0,1:T(8,128)(2,1)} %collective-permute-done.3), channel_id=1, source_target_pairs={{0,3},{1,2},{2,1},{3,0},{4,5},{5,4},{6,7},{7,6},{8,11},{9,10},{10,... | collective-permute-start | bytes 184328 | tf_op jit(solution)/shard_map/ppermute | solution.py:247
  139.1 15.2 %collective-permute-start.12 = (bf16[512,1024]{1,0:T(8,128)(2,1)}, bf16[512,1024]{1,0:T(8,128)(2,1)}, u32[]{:S(2)}, u32[]{:S(2)}) collective-permute-start(bf16[512,1024]{1,0:T(8,128)(2,1)} %shard_map.115), channel_id=1, source_target_pairs={{0,3},{1,2},{2,1},{3,0},{4,5},{5,4},{6,7},{7,6},{8,11},{9,10},{10,... | collective-permute-start | bytes 3145736 | tf_op jit(solution)/shard_map/ppermute | solution.py:247
  140.9 34.6 %collective-permute-start.9 = (bf16[512,1024]{1,0:T(8,128)(2,1)}, bf16[512,1024]{1,0:T(8,128)(2,1)}, u32[]{:S(2)}, u32[]{:S(2)}) collective-permute-start(bf16[512,1024]{1,0:T(8,128)(2,1)} %bitcast.15.x_in), channel_id=1, source_target_pairs={{0,3},{1,2},{2,1},{3,0},{4,5},{5,4},{6,7},{7,6},{8,11},{9,10},{10,... | collective-permute-start | bytes 3145736 | tf_op jit(solution)/shard_map/ppermute | solution.py:247
  158.1 47.2 %all-to-all-start.3 = ((bf16[64,8,1024]{2,1,0:T(8,128)(2,1)}), bf16[64,8,1024]{2,1,0:T(8,128)(2,1)}, u32[]{:S(2)}, u32[]{:S(2)}) async-start(bf16[64,8,1024]{2,1,0:T(8,128)(2,1)} %bitcast.68), calls=%async_computation.3 | async-start | bytes 2097152 | tf_op jit(solution)/shard_map/all_to_all | solution.py:313
  184.1 17.5 %collective-permute-start.10 = (bf16[512,1024]{1,0:T(8,128)(2,1)}, bf16[512,1024]{1,0:T(8,128)(2,1)}, u32[]{:S(2)}, u32[]{:S(2)}) collective-permute-start(bf16[512,1024]{1,0:T(8,128)(2,1)} %shard_map.111), channel_id=1, source_target_pairs={{0,3},{1,2},{2,1},{3,0},{4,5},{5,4},{6,7},{7,6},{8,11},{9,10},{10,... | collective-permute-start | bytes 3145736 | tf_op jit(solution)/shard_map/ppermute | solution.py:247
  205.3 40.6 %all-to-all-start.1 = ((bf16[64,8,1024]{2,1,0:T(8,128)(2,1)}), bf16[64,8,1024]{2,1,0:T(8,128)(2,1)}, u32[]{:S(2)}, u32[]{:S(2)}) async-start(bf16[64,8,1024]{2,1,0:T(8,128)(2,1)} %bitcast.67), calls=%async_computation.1 | async-start | bytes 2097152 | tf_op jit(solution)/shard_map/all_to_all | solution.py:313
  249.6 7.2 %collective-permute-start.14 = (bf16[256,512]{1,0:T(8,128)(2,1)}, bf16[256,512]{1,0:T(8,128)(2,1)S(1)}, u32[]{:S(2)}, u32[]{:S(2)}) collective-permute-start(bf16[256,512]{1,0:T(8,128)(2,1)} %get-tuple-element.24), channel_id=1, source_target_pairs={{0,3},{1,2},{2,1},{3,0},{4,5},{5,4},{6,7},{7,6},{8,11},{9,10},{10,... | collective-permute-start | bytes 786440 | tf_op jit(solution)/shard_map/ppermute | solution.py:247
  252.9 9.5 %collective-permute-start.13 = (bf16[256,512]{1,0:T(8,128)(2,1)}, bf16[256,512]{1,0:T(8,128)(2,1)S(1)}, u32[]{:S(2)}, u32[]{:S(2)}) collective-permute-start(bf16[256,512]{1,0:T(8,128)(2,1)} %get-tuple-element.22), channel_id=1, source_target_pairs={{0,3},{1,2},{2,1},{3,0},{4,5},{5,4},{6,7},{7,6},{8,11},{9,10},{10,... | collective-permute-start | bytes 786440 | tf_op jit(solution)/shard_map/ppermute | solution.py:247
  257.9 8.8 %collective-permute-start.15 = (bf16[256,512]{1,0:T(8,128)(2,1)S(1)}, bf16[256,512]{1,0:T(8,128)(2,1)S(1)}, u32[]{:S(2)}, u32[]{:S(2)}) collective-permute-start(bf16[256,512]{1,0:T(8,128)(2,1)S(1)} %add_convert_fusion.1), channel_id=1, source_target_pairs={{0,1},{1,0},{2,3},{3,2},{4,7},{5,6},{6,5},{7,4},{8,9},{9,8},{10,11... | collective-permute-start | bytes 786440 | tf_op jit(solution)/shard_map/ppermute | solution.py:244
  (4 other events, 38.3 us)

commit v3 on v2

--- a/solution.py
+++ b/solution.py
@@ -1,3 +1,5 @@
+import functools
+
 import jax
 import jax.numpy as jnp
 from jax import lax
@@ -46,12 +48,13 @@
     return [(r, target.at[pl.ds(i * units, units)]) for i, r in enumerate(refs)]
 
 
-def ffn_kernel(gain, x_in, gate_a, gate_b, up_a, up_b, down_a, down_b, out, xv, x, gate_w, up_w, down_w, y, sems):
+def ffn_kernel(gain_in, x_in, gate_a, gate_b, up_a, up_b, down_a, down_b, out, gain, xv, x, gate_w, up_w, down_w, y, sems):
     rows, full = x.shape
     half = full // 2
-    load([(x_in, xv)], sems)[0].wait()
-    pairs = halves((gate_a, gate_b), gate_w) + halves((up_a, up_b), up_w) + halves((down_a, down_b), down_w)
-    copies = load(pairs, sems)
+    pairs = [(x_in, xv), (gain_in, gain), *halves((gate_a, gate_b), gate_w), *halves((up_a, up_b), up_w)]
+    copies = load(pairs + halves((down_a, down_b), down_w), sems)
+    for c in copies[:2]:
+        c.wait()
     small = 32
     first = lax.broadcasted_iota(jnp.int32, (small // 8, 8, half), 1) < 4
 
@@ -71,14 +74,14 @@
         return carry
 
     lax.fori_loop(0, rows // small, norm_step, 0)
-    for c in copies[:2]:
+    for c in copies[2:4]:
         c.wait()
     gate = dot(x[...], gate_w[...], ((1,), (1,)))
-    for c in copies[2:4]:
+    for c in copies[4:6]:
         c.wait()
     up = dot(x[...], up_w[...], ((1,), (1,)))
     hidden = (gate / (1.0 + jnp.exp(-gate)) * up).astype(BF16)
-    for c in copies[4:]:
+    for c in copies[6:]:
         c.wait()
     y[...] = dot(hidden, down_w[...])
 
@@ -97,19 +100,20 @@
     lax.fori_loop(0, rows // small, out_step, 0)
 
 
-def half_ffn(gain, x, weights, dtype):
+def half_ffn(gain, x, weights):
     (rows, full), units = (x.shape[0] // 2, x.shape[1] * 2), 2 * weights[0].shape[0]
     return pl.pallas_call(
         ffn_kernel,
-        out_shape=jax.ShapeDtypeStruct(x.shape, dtype),
-        in_specs=[VMEM] + [HBM] * 7,
+        out_shape=jax.ShapeDtypeStruct(x.shape, BF16),
+        in_specs=[HBM] * 8,
         out_specs=VMEM,
         scratch_shapes=[
+            pltpu.VMEM(gain.shape, F32),
             pltpu.VMEM(x.shape, BF16),
             pltpu.VMEM((rows, full), BF16),
             *[pltpu.VMEM((units, full), BF16)] * 3,
             pltpu.VMEM((rows, full), F32),
-            pltpu.SemaphoreType.DMA((6,)),
+            pltpu.SemaphoreType.DMA((8,)),
         ],
         cost_estimate=pl.CostEstimate(
             flops=6 * rows * full * units,
@@ -149,24 +153,6 @@
     )(starts, pick, *parts)
 
 
-def join_kernel(kept, got, out):
-    out[...] = (kept[...] + got[...].astype(F32)).astype(BF16)
-
-
-def joined(kept, got):
-    rows, half = kept.shape
-    block = pl.BlockSpec((rows // 4, half), lambda i: (i, 0))
-    return pl.pallas_call(
-        join_kernel,
-        out_shape=jax.ShapeDtypeStruct(kept.shape, BF16),
-        grid=(4,),
-        in_specs=[block] * 2,
-        out_specs=block,
-        cost_estimate=pl.CostEstimate(flops=kept.size, transcendentals=0, bytes_accessed=8 * kept.size),
-        compiler_params=BIG,
-    )(kept, got)
-
-
 def gather_kernel(mix_hi, mix_lo, rows, base, out):
     half = rows.shape[1]
     for h in range(2):
@@ -187,9 +173,9 @@
     )(mix_hi, mix_lo, rows, base)
 
 
-def combine_kernel(starts, mix_hi, mix_lo, rows, base, *outs):
+def combine_kernel(starts, mix_hi, mix_lo, rows, base, *outs, parts):
     width, half = outs[0].shape[1], rows.shape[1]
-    for k, out in enumerate(outs):
+    for k, out in zip(parts, outs):
         h = starts[k] // half
         from_rows = pl.ds(pl.multiple_of(starts[k] % half, width), width)
         value = dot(mix_hi[h], rows[:, from_rows]) + dot(mix_lo[h], rows[:, from_rows])
@@ -197,11 +183,11 @@
         out[...] = (base[:, at] + value).astype(out.dtype)
 
 
-def combined(starts, mix_hi, mix_lo, rows, base, dtype):
+def combined(starts, parts, mix_hi, mix_lo, rows, base, dtype):
     tokens, full = base.shape
-    count = starts.shape[0]
+    count = len(parts)
     return pl.pallas_call(
-        combine_kernel,
+        functools.partial(combine_kernel, parts=parts),
         out_shape=[jax.ShapeDtypeStruct((tokens, full // 4), dtype)] * count,
         in_specs=[SMEM] + [VMEM] * 4,
         out_specs=[VMEM] * count,
@@ -306,17 +292,17 @@
             arrived = lax.all_to_all(there, "ep", 0, 0, tiled=True)
             arrived = arrived.reshape(outgoing[c].shape)
             arrived_far = to_across(arrived)
-            sent = half_ffn(gain, arrived_far, weights, BF16)
+            sent = half_ffn(gain, arrived_far, weights)
             got = to_across(sent)
-            kept = half_ffn(gain, arrived, weights, F32)
-            out = joined(kept, got).reshape(there.shape)
+            kept = half_ffn(gain, arrived, weights)
+            out = (kept.astype(F32) + got.astype(F32)).astype(BF16).reshape(there.shape)
             returned = lax.all_to_all(out, "ep", 0, 0, tiled=True)
             returned = returned.reshape(outgoing[c].shape)
             if c < CHUNKS - 1:
                 acc = gathered(*mixes[c], returned, acc)
             else:
-                for_diag, for_across = combined(starts[:1:-1], *mixes[c], returned, acc, BF16)
-                total_near, total_me = combined(starts[1::-1], *mixes[c], returned, acc, F32)
+                for_diag, for_across = combined(starts, (3, 2), *mixes[c], returned, acc, BF16)
+                total_near, total_me = combined(starts, (1, 0), *mixes[c], returned, acc, F32)
         came_near = to_across(for_diag)
         came_me = to_across(for_across)
         again = to_near((total_near + came_near.astype(F32)).astype(BF16))

time: 272 us -> 225 us (0.83)
  waiting for transfers between devices: 105 us -> 68.5 us
  Pallas kernels: 61.1 us -> 48.2 us
  other arithmetic: 8.75 us -> 15.3 us
    ppermute x6, waiting for transfers between devices: 55.8 us -> 23 us  [to_near(): return lax.ppermute(value, BOTH, near_pairs)]
    pallas_call x8 -> x6, Pallas kernels: 50 us -> 37 us  [the longest x4 29.5 us: half_ffn(): pl.pallas_call(ffn_kernel, out_shape=jax.ShapeDtypeStruct(x.shape, BF16),...]
    all_to_all x2, waiting for transfers between devices: 17.7 us -> 11.6 us  [body(): returned = lax.all_to_all(out, 'ep', 0, 0, tiled=True)]
    reshape x0 -> x2, other arithmetic: none -> 5.64 us  [body(): out = (kept.astype(F32) + got.astype(F32)).astype(BF16).reshape(there.shape)]
    ppermute x10, waiting for transfers between devices: 5.88 us -> 11.5 us  [to_across(): return lax.ppermute(value, BOTH, across_pairs)]
    all_to_all x2, waiting for transfers between devices: 25.3 us -> 22.4 us  [body(): arrived = lax.all_to_all(there, 'ep', 0, 0, tiled=True)]
  transfers between devices with their start and end apart: 20 -> 20, of which waited for: 8 -> 10; matrix products, arithmetic and copies ran while one was open for 11% -> 15% of each run, Pallas kernels for 20% -> 19%
where the time goes in v3:
time: 225 us; the launch traced here: 223 us
  waiting for transfers between devices  68.5 us (30%)
  starting transfers between devices  61.5 us (27%)
  Pallas kernels  48.2 us (21%)
  matrix products  16.7 us (7%)
  other arithmetic  15.3 us (7%)
  between operations  7.69 us (3%)
  local copies, waits for them, and re-layouts  4.66 us (2%)
    pallas_call x4, Pallas kernels, half_ffn(): pl.pallas_call(ffn_kernel, out_shape=jax.ShapeDtypeStruct(x.shape, BF16),...  29.5 us
    ppermute x6, waiting for transfers between devices, to_near(): return lax.ppermute(value, BOTH, near_pairs)  23 us
    all_to_all x2, waiting for transfers between devices, body(): arrived = lax.all_to_all(there, 'ep', 0, 0, tiled=True)  22.4 us
    all_to_all x2, starting transfers between devices, body(): returned = lax.all_to_all(out, 'ep', 0, 0, tiled=True)  20.4 us
    all_to_all x2, starting transfers between devices, body(): arrived = lax.all_to_all(there, 'ep', 0, 0, tiled=True)  17.8 us
    dot_general x12, matrix products, dot(): return lax.dot_general(a, b, (dims, ((), ())), preferred_element_type=F32)  16.7 us
    ppermute x10, starting transfers between devices, to_across(): return lax.ppermute(value, BOTH, across_pairs)  12.4 us
    all_to_all x2, waiting for transfers between devices, body(): returned = lax.all_to_all(out, 'ep', 0, 0, tiled=True)  11.6 us
  transfers between devices with their start and end apart: 20, of which 10 were waited for; matrix products, arithmetic and copies ran while one was open for 15% of the time, Pallas kernels for 19%

profile of v3, /device:TPU:8, one launch (start us, length us, event | category | flops | bytes accessed | tf_op | source)
XLA Modules:
  0.0 222.6 jit_solution(12697972883498588807)
XLA Ops:
  4.4 5.1 %collective-permute-done.part_1 = bf16[256,512]{1,0:T(8,128)(2,1)} collective-permute-done((bf16[256,512]{1,0:T(8,128)(2,1)}, bf16[256,512]{1,0:T(8,128)(2,1)}, u32[]{:S(2)}, u32[]{:S(2)}) %collective-permute-start) | collective-permute-done | bytes 262176 | tf_op jit(solution)/shard_map/ppermute | solution.py:230
  11.5 4.5 %collective-permute-done.2.part_3 = bf16[256,512]{1,0:T(8,128)(2,1)S(1)} collective-permute-done((bf16[256,512]{1,0:T(8,128)(2,1)}, bf16[256,512]{1,0:T(8,128)(2,1)S(1)}, u32[]{:S(2)}, u32[]{:S(2)}) %collective-permute-start.2) | collective-permute-done | bytes 262176 | tf_op jit(solution)/shard_map/ppermute | solution.py:233
  16.7 3.0 %shard_map.112 = bf16[512,1024]{1,0:T(8,128)(2,1)} custom-call(s32[4]{0:T(128)} %add_multiply_fusion.starts, bf16[512,256]{1,0:T(8,128)(2,1)} %get-tuple-element.29.pick, bf16[256,512]{1,0:T(8,128)(2,1)} %part_0.3, bf16[256,512]{1,0:T(8,128)(2,1)} %collective-permute-done.part_1, bf16[256,512]{1,0:T(8,128)(2,1)} %collective-permute-done.1.part_2, ...), custom_call_target="tpu_custom_call" | custom-call | flops 536870912 | bytes 2097152 | tf_op jit(solution)/shard_map/pallas_call | solution.py:144
  19.7 11.9 %all-to-all-start.2 = ((bf16[64,8,1024]{2,1,0:T(8,128)(2,1)}), bf16[64,8,1024]{2,1,0:T(8,128)(2,1)}, u32[]{:S(2)}, u32[]{:S(2)}) async-start(bf16[64,8,1024]{2,1,0:T(8,128)(2,1)} %bitcast.68), calls=%async_computation.2 | async-start | bytes 2097152 | tf_op jit(solution)/shard_map/all_to_all | solution.py:292
  34.6 3.4 %shard_map.109 = (bf16[512,1024]{1,0:T(8,128)(2,1)}, bf16[256,2048]{1,0:T(8,128)(2,1)}) custom-call(s32[4]{0:T(128)} %add_multiply_fusion.starts, bf16[512,256]{1,0:T(8,128)(2,1)} %get-tuple-element.30.pick, bf16[256,512]{1,0:T(8,128)(2,1)} %part_0.3, bf16[256,512]{1,0:T(8,128)(2,1)} %collective-permute-done.part_1, ...), custom_call_target="tpu_custom_call" | custom-call | flops 536870912 | bytes 2097152 | tf_op jit(solution)/shard_map/pallas_call | solution.py:144
  38.0 22.4 %all-to-all-done.2 = bf16[64,8,1024]{2,1,0:T(8,128)(2,1)} async-done(((bf16[64,8,1024]{2,1,0:T(8,128)(2,1)}), bf16[64,8,1024]{2,1,0:T(8,128)(2,1)}, u32[]{:S(2)}, u32[]{:S(2)}) %all-to-all-start.2) | async-done | bytes 1048608 | tf_op jit(solution)/shard_map/all_to_all | solution.py:292
  60.4 5.8 %all-to-all-start = ((bf16[64,8,1024]{2,1,0:T(8,128)(2,1)}), bf16[64,8,1024]{2,1,0:T(8,128)(2,1)}, u32[]{:S(2)}, u32[]{:S(2)}) async-start(bf16[64,8,1024]{2,1,0:T(8,128)(2,1)} %bitcast.69), calls=%async_computation | async-start | bytes 2097152 | tf_op jit(solution)/shard_map/all_to_all | solution.py:292
  80.4 13.6 %collective-permute-done.3 = bf16[512,60]{0,1:T(8,128)(2,1)} collective-permute-done((bf16[512,60]{0,1:T(8,128)(2,1)S(1)}, bf16[512,60]{0,1:T(8,128)(2,1)}, u32[]{:S(2)}, u32[]{:S(2)}) %collective-permute-start.3) | collective-permute-done | bytes 61472 | tf_op jit(solution)/shard_map/ppermute | solution.py:230
  96.0 7.4 %shard_map.114 = bf16[512,1024]{1,0:T(8,128)(2,1)} custom-call(f32[1,2048]{1,0:T(1,128)} %bitcast.70, bf16[512,1024]{1,0:T(8,128)(2,1)} %collective-permute-done.11.x_in, bf16[352,2048]{1,0:T(8,128)(2,1)} %bitcast.54, bf16[352,2048]{1,0:T(8,128)(2,1)} %collective-permute-done.6.gate_b, bf16[352,2048]{1,0:T(8,128)(2,1)} %bitcast.59, ...), custom_call_target="tpu_custom_call" | custom-call | flops 2214592512 | bytes 10747904 | tf_op jit(solution)/shard_map/pallas_call | solution.py:105
  108.2 7.4 %shard_map.113 = bf16[512,1024]{1,0:T(8,128)(2,1)} custom-call(f32[1,2048]{1,0:T(1,128)} %bitcast.71, bf16[512,1024]{1,0:T(8,128)(2,1)} %bitcast.27.x_in, bf16[352,2048]{1,0:T(8,128)(2,1)} %bitcast.55, bf16[352,2048]{1,0:T(8,128)(2,1)} %collective-permute-done.6.gate_b, bf16[352,2048]{1,0:T(8,128)(2,1)} %bitcast.60, ...), custom_call_target="tpu_custom_call" | custom-call | flops 2214592512 | bytes 10747904 | tf_op jit(solution)/shard_map/pallas_call | solution.py:105
  115.5 3.1 %collective-permute-done.12 = bf16[512,1024]{1,0:T(8,128)(2,1)} collective-permute-done((bf16[512,1024]{1,0:T(8,128)(2,1)}, bf16[512,1024]{1,0:T(8,128)(2,1)}, u32[]{:S(2)}, u32[]{:S(2)}) %collective-permute-start.12) | collective-permute-done | bytes 1048608 | tf_op jit(solution)/shard_map/ppermute | solution.py:233
  118.7 2.9 %fusion.7 = bf16[64,8,1024]{2,1,0:T(8,128)(2,1)} fusion(bf16[512,1024]{1,0:T(8,128)(2,1)} %collective-permute-done.12, bf16[512,1024]{1,0:T(8,128)(2,1)} %shard_map.113), kind=kLoop, calls=%fused_computation.17 | loop fusion | flops 2097152 | bytes 3145728 | tf_op jit(solution)/shard_map/reshape | solution.py:298
  121.6 10.5 %all-to-all-start.3 = ((bf16[64,8,1024]{2,1,0:T(8,128)(2,1)}), bf16[64,8,1024]{2,1,0:T(8,128)(2,1)}, u32[]{:S(2)}, u32[]{:S(2)}) async-start(bf16[64,8,1024]{2,1,0:T(8,128)(2,1)} %fusion.7), calls=%async_computation.3 | async-start | bytes 2097152 | tf_op jit(solution)/shard_map/all_to_all | solution.py:299
  134.6 7.4 %shard_map.111 = bf16[512,1024]{1,0:T(8,128)(2,1)} custom-call(f32[1,2048]{1,0:T(1,128)} %bitcast.72, bf16[512,1024]{1,0:T(8,128)(2,1)} %collective-permute-done.9.x_in, bf16[352,2048]{1,0:T(8,128)(2,1)} %bitcast.56, bf16[352,2048]{1,0:T(8,128)(2,1)} %collective-permute-done.6.gate_b, bf16[352,2048]{1,0:T(8,128)(2,1)} %bitcast.61, ...), custom_call_target="tpu_custom_call" | custom-call | flops 2214592512 | bytes 10747904 | tf_op jit(solution)/shard_map/pallas_call | solution.py:105
  146.9 7.3 %shard_map.110 = bf16[512,1024]{1,0:T(8,128)(2,1)} custom-call(f32[1,2048]{1,0:T(1,128)} %bitcast.73, bf16[512,1024]{1,0:T(8,128)(2,1)} %bitcast.15.x_in, bf16[352,2048]{1,0:T(8,128)(2,1)} %bitcast.57, bf16[352,2048]{1,0:T(8,128)(2,1)} %collective-permute-done.6.gate_b, bf16[352,2048]{1,0:T(8,128)(2,1)} %bitcast.62, ...), custom_call_target="tpu_custom_call" | custom-call | flops 2214592512 | bytes 10747904 | tf_op jit(solution)/shard_map/pallas_call | solution.py:105
  154.2 3.1 %collective-permute-done.10 = bf16[512,1024]{1,0:T(8,128)(2,1)S(1)} collective-permute-done((bf16[512,1024]{1,0:T(8,128)(2,1)}, bf16[512,1024]{1,0:T(8,128)(2,1)S(1)}, u32[]{:S(2)}, u32[]{:S(2)}) %collective-permute-start.10) | collective-permute-done | bytes 1048608 | tf_op jit(solution)/shard_map/ppermute | solution.py:233
  160.8 9.9 %all-to-all-start.1 = ((bf16[64,8,1024]{2,1,0:T(8,128)(2,1)}), bf16[64,8,1024]{2,1,0:T(8,128)(2,1)}, u32[]{:S(2)}, u32[]{:S(2)}) async-start(bf16[64,8,1024]{2,1,0:T(8,128)(2,1)} %fusion.6), calls=%async_computation.1 | async-start | bytes 2097152 | tf_op jit(solution)/shard_map/all_to_all | solution.py:299
  176.8 6.9 %convolution_multiply_fusion.base = f32[256,2048]{1,0:T(8,128)} fusion(bf16[704,2048]{1,0:T(8,128)(2,1)S(1)} %copy-done, f32[256]{0:T(256)S(1)} %add_divide_fusion, f32[256,704]{0,1:T(8,128)} %fusion.48, bf16[256,2048]{1,0:T(8,128)(2,1)} %fusion.2, bf16[2048,704]{0,1:T(8,128)(2,1)} %param.20), kind=kOutput, calls=%fused_computation | convolution fusion | flops 1478000640 | bytes 9634816 | tf_op jit(solution)/shard_map/dot_general | solution.py:30
  183.7 4.8 %shard_map.115.base = f32[256,2048]{1,0:T(8,128)} custom-call(bf16[2,256,512]{2,1,0:T(8,128)(2,1)} %get-tuple-element.19.mix_hi, bf16[2,256,512]{2,1,0:T(8,128)(2,1)} %get-tuple-element.20.mix_lo, bf16[512,1024]{1,0:T(8,128)(2,1)} %bitcast.29.rows, f32[256,2048]{1,0:T(8,128)} %convolution_multiply_fusion.base), custom_call_target="tpu_custom_call" | custom-call | flops 1073741824 | bytes 4194304 | tf_op jit(solution)/shard_map/pallas_call | solution.py:164
  188.6 10.8 %all-to-all-done.1 = bf16[64,8,1024]{2,1,0:T(8,128)(2,1)} async-done(((bf16[64,8,1024]{2,1,0:T(8,128)(2,1)}), bf16[64,8,1024]{2,1,0:T(8,128)(2,1)}, u32[]{:S(2)}, u32[]{:S(2)}) %all-to-all-start.1) | async-done | bytes 1048608 | tf_op jit(solution)/shard_map/all_to_all | solution.py:299
  199.4 3.7 %shard_map.117 = (bf16[256,512]{1,0:T(8,128)(2,1)}, bf16[256,512]{1,0:T(8,128)(2,1)}) custom-call(s32[4]{0:T(128)} %add_multiply_fusion.starts, bf16[2,256,512]{2,1,0:T(8,128)(2,1)} %get-tuple-element.16.mix_hi, bf16[2,256,512]{2,1,0:T(8,128)(2,1)} %get-tuple-element.17.mix_lo, bf16[512,1024]{1,0:T(8,128)(2,1)} %bitcast.24.rows, f32[256,2048]{1,0:T(8,128)} %shard_map.115.base), custom_call_target="tpu_custom_call" | custom-call | flops 536870912 | bytes 4194304 | tf_op jit(solution)/shard_map/pallas_call | solution.py:189
  205.7 3.8 %shard_map.116 = (f32[256,512]{1,0:T(8,128)}, f32[256,512]{1,0:T(8,128)}) custom-call(s32[4]{0:T(128)} %add_multiply_fusion.starts, bf16[2,256,512]{2,1,0:T(8,128)(2,1)} %get-tuple-element.16.mix_hi, bf16[2,256,512]{2,1,0:T(8,128)(2,1)} %get-tuple-element.17.mix_lo, bf16[512,1024]{1,0:T(8,128)(2,1)} %bitcast.24.rows, f32[256,2048]{1,0:T(8,128)} %shard_map.115.base), custom_call_target="tpu_custom_call" | custom-call | flops 536870912 | bytes 4194304 | tf_op jit(solution)/shard_map/pallas_call | solution.py:189
  211.3 5.1 %collective-permute-start.15 = (bf16[256,512]{1,0:T(8,128)(2,1)S(1)}, bf16[256,512]{1,0:T(8,128)(2,1)S(1)}, u32[]{:S(2)}, u32[]{:S(2)}) collective-permute-start(bf16[256,512]{1,0:T(8,128)(2,1)S(1)} %add_convert_fusion.3), channel_id=1, source_target_pairs={{0,1},{1,0},{2,3},{3,2},{4,7},{5,6},{6,5},{7,4},{8,9},{9,8},{10,11... | collective-permute-start | bytes 786440 | tf_op jit(solution)/shard_map/ppermute | solution.py:230
  216.4 4.3 %collective-permute-done.15 = bf16[256,512]{1,0:T(8,128)(2,1)S(1)} collective-permute-done((bf16[256,512]{1,0:T(8,128)(2,1)S(1)}, bf16[256,512]{1,0:T(8,128)(2,1)S(1)}, u32[]{:S(2)}, u32[]{:S(2)}) %collective-permute-start.15) | collective-permute-done | bytes 262176 | tf_op jit(solution)/shard_map/ppermute | solution.py:230
  (84 shorter events, 46.7 us)
Async XLA Ops:
  0.0 176.8 %copy-start = (bf16[704,2048]{1,0:T(8,128)(2,1)S(1)}, bf16[704,2048]{1,0:T(8,128)(2,1)}, u32[]{:S(2)}) copy-start(bf16[704,2048]{1,0:T(8,128)(2,1)} %param.21) | copy-start | bytes 8650756
  0.0 9.4 %collective-permute-start = (bf16[256,512]{1,0:T(8,128)(2,1)}, bf16[256,512]{1,0:T(8,128)(2,1)}, u32[]{:S(2)}, u32[]{:S(2)}) collective-permute-start(bf16[256,512]{1,0:T(8,128)(2,1)} %part_0.3), channel_id=1, source_target_pairs={{0,1},{1,0},{2,3},{3,2},{4,7},{5,6},{6,5},{7,4},{8,9},{9,8},{10,11... | collective-permute-start | bytes 786440 | tf_op jit(solution)/shard_map/ppermute | solution.py:230
  2.2 9.3 %collective-permute-start.1 = (bf16[256,512]{1,0:T(8,128)(2,1)}, bf16[256,512]{1,0:T(8,128)(2,1)}, u32[]{:S(2)}, u32[]{:S(2)}) collective-permute-start(bf16[256,512]{1,0:T(8,128)(2,1)} %part_0.3), channel_id=1, source_target_pairs={{0,3},{1,2},{2,1},{3,0},{4,5},{5,4},{6,7},{7,6},{8,11},{9,10},{10,... | collective-permute-start | bytes 786440 | tf_op jit(solution)/shard_map/ppermute | solution.py:233
  9.4 6.6 %collective-permute-start.2 = (bf16[256,512]{1,0:T(8,128)(2,1)}, bf16[256,512]{1,0:T(8,128)(2,1)S(1)}, u32[]{:S(2)}, u32[]{:S(2)}) collective-permute-start(bf16[256,512]{1,0:T(8,128)(2,1)} %collective-permute-done.part_1), channel_id=1, source_target_pairs={{0,3},{1,2},{2,1},{3,0},{4,5},{5,4},{6,7},{7,6},{8,11},{9,10},{10,... | collective-permute-start | bytes 786440 | tf_op jit(solution)/shard_map/ppermute | solution.py:233
  19.7 40.6 %all-to-all-start.2 = ((bf16[64,8,1024]{2,1,0:T(8,128)(2,1)}), bf16[64,8,1024]{2,1,0:T(8,128)(2,1)}, u32[]{:S(2)}, u32[]{:S(2)}) async-start(bf16[64,8,1024]{2,1,0:T(8,128)(2,1)} %bitcast.68), calls=%async_computation.2 | async-start | bytes 2097152 | tf_op jit(solution)/shard_map/all_to_all | solution.py:292
  31.7 34.6 %copy-start.7 = (bf16[512,60]{0,1:T(8,128)(2,1)S(1)}, bf16[512,60]{0,1:T(8,128)(2,1)}, u32[]{:S(2)}) copy-start(bf16[512,60]{0,1:T(8,128)(2,1)} %param.13) | copy-start | bytes 184324
  31.7 38.0 %copy-start.8 = (s32[4]{0:T(128)S(1)}, s32[4]{0:T(128)}, u32[]{:S(2)}) copy-start(s32[4]{0:T(128)} %add_multiply_fusion.starts) | copy-start | bytes 52
  31.7 43.6 %copy-start.9 = (bf16[2048]{0:T(1024)(128)(2,1)S(1)}, bf16[2048]{0:T(1024)(128)(2,1)}, u32[]{:S(2)}) copy-start(bf16[2048]{0:T(1024)(128)(2,1)} %param.14) | copy-start | bytes 12292
  31.7 63.6 %collective-permute-start.6 = (bf16[352,2048]{1,0:T(8,128)(2,1)}, bf16[352,2048]{1,0:T(8,128)(2,1)}, u32[]{:S(2)}, u32[]{:S(2)}) collective-permute-start(bf16[352,2048]{1,0:T(8,128)(2,1)} %bitcast.53), channel_id=1, source_target_pairs={{0,1},{1,0},{2,3},{3,2},{4,7},{5,6},{6,5},{7,4},{8,9},{9,8},{10,11... | collective-permute-start | bytes 4325384 | tf_op jit(solution)/shard_map/ppermute | solution.py:230
  32.5 63.4 %collective-permute-start.7 = (bf16[352,2048]{1,0:T(8,128)(2,1)}, bf16[352,2048]{1,0:T(8,128)(2,1)}, u32[]{:S(2)}, u32[]{:S(2)}) collective-permute-start(bf16[352,2048]{1,0:T(8,128)(2,1)} %bitcast.58), channel_id=1, source_target_pairs={{0,1},{1,0},{2,3},{3,2},{4,7},{5,6},{6,5},{7,4},{8,9},{9,8},{10,11... | collective-permute-start | bytes 4325384 | tf_op jit(solution)/shard_map/ppermute | solution.py:230
  33.8 62.2 %collective-permute-start.8 = (bf16[352,2048]{1,0:T(8,128)(2,1)}, bf16[352,2048]{1,0:T(8,128)(2,1)}, u32[]{:S(2)}, u32[]{:S(2)}) collective-permute-start(bf16[352,2048]{1,0:T(8,128)(2,1)} %bitcast.63), channel_id=1, source_target_pairs={{0,1},{1,0},{2,3},{3,2},{4,7},{5,6},{6,5},{7,4},{8,9},{9,8},{10,11... | collective-permute-start | bytes 4325384 | tf_op jit(solution)/shard_map/ppermute | solution.py:230
  60.4 45.9 %all-to-all-start = ((bf16[64,8,1024]{2,1,0:T(8,128)(2,1)}), bf16[64,8,1024]{2,1,0:T(8,128)(2,1)}, u32[]{:S(2)}, u32[]{:S(2)}) async-start(bf16[64,8,1024]{2,1,0:T(8,128)(2,1)} %bitcast.69), calls=%async_computation | async-start | bytes 2097152 | tf_op jit(solution)/shard_map/all_to_all | solution.py:292
  66.2 27.7 %collective-permute-start.3 = (bf16[512,60]{0,1:T(8,128)(2,1)S(1)}, bf16[512,60]{0,1:T(8,128)(2,1)}, u32[]{:S(2)}, u32[]{:S(2)}) collective-permute-start(bf16[512,60]{0,1:T(8,128)(2,1)S(1)} %copy-done.7), channel_id=1, source_target_pairs={{0,1},{1,0},{2,3},{3,2},{4,7},{5,6},{6,5},{7,4},{8,9},{9,8},{10,11... | collective-permute-start | bytes 184328 | tf_op jit(solution)/shard_map/ppermute | solution.py:230
  67.1 28.9 %collective-permute-start.11 = (bf16[512,1024]{1,0:T(8,128)(2,1)}, bf16[512,1024]{1,0:T(8,128)(2,1)}, u32[]{:S(2)}, u32[]{:S(2)}) collective-permute-start(bf16[512,1024]{1,0:T(8,128)(2,1)} %bitcast.27.x_in), channel_id=1, source_target_pairs={{0,3},{1,2},{2,1},{3,0},{4,5},{5,4},{6,7},{7,6},{8,11},{9,10},{10,... | collective-permute-start | bytes 3145736 | tf_op jit(solution)/shard_map/ppermute | solution.py:233
  93.9 39.4 %collective-permute-start.4 = (bf16[512,60]{0,1:T(8,128)(2,1)S(1)}, bf16[512,60]{0,1:T(8,128)(2,1)}, u32[]{:S(2)}, u32[]{:S(2)}) collective-permute-start(bf16[512,60]{0,1:T(8,128)(2,1)S(1)} %copy-done.7), channel_id=1, source_target_pairs={{0,3},{1,2},{2,1},{3,0},{4,5},{5,4},{6,7},{7,6},{8,11},{9,10},{10,... | collective-permute-start | bytes 184328 | tf_op jit(solution)/shard_map/ppermute | solution.py:233
  95.3 48.4 %collective-permute-start.5 = (bf16[512,60]{0,1:T(8,128)(2,1)}, bf16[512,60]{0,1:T(8,128)(2,1)}, u32[]{:S(2)}, u32[]{:S(2)}) collective-permute-start(bf16[512,60]{0,1:T(8,128)(2,1)} %collective-permute-done.3), channel_id=1, source_target_pairs={{0,3},{1,2},{2,1},{3,0},{4,5},{5,4},{6,7},{7,6},{8,11},{9,10},{10,... | collective-permute-start | bytes 184328 | tf_op jit(solution)/shard_map/ppermute | solution.py:233
  103.5 15.2 %collective-permute-start.12 = (bf16[512,1024]{1,0:T(8,128)(2,1)}, bf16[512,1024]{1,0:T(8,128)(2,1)}, u32[]{:S(2)}, u32[]{:S(2)}) collective-permute-start(bf16[512,1024]{1,0:T(8,128)(2,1)} %shard_map.114), channel_id=1, source_target_pairs={{0,3},{1,2},{2,1},{3,0},{4,5},{5,4},{6,7},{7,6},{8,11},{9,10},{10,... | collective-permute-start | bytes 3145736 | tf_op jit(solution)/shard_map/ppermute | solution.py:233
  106.2 28.4 %collective-permute-start.9 = (bf16[512,1024]{1,0:T(8,128)(2,1)}, bf16[512,1024]{1,0:T(8,128)(2,1)}, u32[]{:S(2)}, u32[]{:S(2)}) collective-permute-start(bf16[512,1024]{1,0:T(8,128)(2,1)} %bitcast.15.x_in), channel_id=1, source_target_pairs={{0,3},{1,2},{2,1},{3,0},{4,5},{5,4},{6,7},{7,6},{8,11},{9,10},{10,... | collective-permute-start | bytes 3145736 | tf_op jit(solution)/shard_map/ppermute | solution.py:233
  121.6 39.2 %all-to-all-start.3 = ((bf16[64,8,1024]{2,1,0:T(8,128)(2,1)}), bf16[64,8,1024]{2,1,0:T(8,128)(2,1)}, u32[]{:S(2)}, u32[]{:S(2)}) async-start(bf16[64,8,1024]{2,1,0:T(8,128)(2,1)} %fusion.7), calls=%async_computation.3 | async-start | bytes 2097152 | tf_op jit(solution)/shard_map/all_to_all | solution.py:299
  142.0 15.3 %collective-permute-start.10 = (bf16[512,1024]{1,0:T(8,128)(2,1)}, bf16[512,1024]{1,0:T(8,128)(2,1)S(1)}, u32[]{:S(2)}, u32[]{:S(2)}) collective-permute-start(bf16[512,1024]{1,0:T(8,128)(2,1)} %shard_map.111), channel_id=1, source_target_pairs={{0,3},{1,2},{2,1},{3,0},{4,5},{5,4},{6,7},{7,6},{8,11},{9,10},{10,... | collective-permute-start | bytes 3145736 | tf_op jit(solution)/shard_map/ppermute | solution.py:233
  160.8 38.6 %all-to-all-start.1 = ((bf16[64,8,1024]{2,1,0:T(8,128)(2,1)}), bf16[64,8,1024]{2,1,0:T(8,128)(2,1)}, u32[]{:S(2)}, u32[]{:S(2)}) async-start(bf16[64,8,1024]{2,1,0:T(8,128)(2,1)} %fusion.6), calls=%async_computation.1 | async-start | bytes 2097152 | tf_op jit(solution)/shard_map/all_to_all | solution.py:299
  203.1 7.1 %collective-permute-start.14 = (bf16[256,512]{1,0:T(8,128)(2,1)}, bf16[256,512]{1,0:T(8,128)(2,1)S(1)}, u32[]{:S(2)}, u32[]{:S(2)}) collective-permute-start(bf16[256,512]{1,0:T(8,128)(2,1)} %get-tuple-element.24), channel_id=1, source_target_pairs={{0,3},{1,2},{2,1},{3,0},{4,5},{5,4},{6,7},{7,6},{8,11},{9,10},{10,... | collective-permute-start | bytes 786440 | tf_op jit(solution)/shard_map/ppermute | solution.py:233
  205.6 10.8 %collective-permute-start.13 = (bf16[256,512]{1,0:T(8,128)(2,1)}, bf16[256,512]{1,0:T(8,128)(2,1)S(1)}, u32[]{:S(2)}, u32[]{:S(2)}) collective-permute-start(bf16[256,512]{1,0:T(8,128)(2,1)} %get-tuple-element.22), channel_id=1, source_target_pairs={{0,3},{1,2},{2,1},{3,0},{4,5},{5,4},{6,7},{7,6},{8,11},{9,10},{10,... | collective-permute-start | bytes 786440 | tf_op jit(solution)/shard_map/ppermute | solution.py:233
  211.3 9.4 %collective-permute-start.15 = (bf16[256,512]{1,0:T(8,128)(2,1)S(1)}, bf16[256,512]{1,0:T(8,128)(2,1)S(1)}, u32[]{:S(2)}, u32[]{:S(2)}) collective-permute-start(bf16[256,512]{1,0:T(8,128)(2,1)S(1)} %add_convert_fusion.3), channel_id=1, source_target_pairs={{0,1},{1,0},{2,3},{3,2},{4,7},{5,6},{6,5},{7,4},{8,9},{9,8},{10,11... | collective-permute-start | bytes 786440 | tf_op jit(solution)/shard_map/ppermute | solution.py:230
  (7 other events, 44.6 us)

commit v4 on v3

--- a/solution.py
+++ b/solution.py
@@ -16,14 +16,15 @@
 
 def pair_perms(mesh):
     ep, tp = mesh.shape["ep"], mesh.shape["tp"]
-    near, across = [], []
+    near, across, diag = [], [], []
     for e in range(ep):
         for t in range(tp):
             flip, mirror = t ^ 1, tp - 1 - t
             a, b = (flip, mirror) if e % 2 == 0 else (mirror, flip)
             near.append((e * tp + t, e * tp + a))
             across.append((e * tp + t, e * tp + b))
-    return near, across
+            diag.append((e * tp + t, e * tp + (t ^ 2)))
+    return near, across, diag
 
 
 def dot(a, b, dims=((1,), (0,))):
@@ -199,7 +200,7 @@
 
 
 def make(mesh):
-    near_pairs, across_pairs = pair_perms(mesh)
+    near_pairs, across_pairs, diag_pairs = pair_perms(mesh)
 
     def body(
         tokens,
@@ -234,7 +235,7 @@
 
         def all_parts(value):
             a, b = to_near(value), to_across(value)
-            return [value, a, b, to_across(a)]
+            return [value, a, b, lax.ppermute(value, BOTH, diag_pairs)]
 
         parts = all_parts(tokens)
         own_w = (w_gate[0].T, w_up[0].T, w_down[0])
@@ -306,7 +307,8 @@
         came_near = to_across(for_diag)
         came_me = to_across(for_across)
         again = to_near((total_near + came_near.astype(F32)).astype(BF16))
-        return (total_me + came_me.astype(F32) + again.astype(F32)).astype(BF16)
+        total_me = lax.optimization_barrier(total_me + came_me.astype(F32))
+        return (total_me + again.astype(F32)).astype(BF16)
 
     return body
 

time: 225 us -> 222 us (0.987)
  waiting for transfers between devices: 68.5 us -> 61.3 us
  starting transfers between devices: 61.5 us -> 65.7 us
    ppermute x6, waiting for transfers between devices: 23 us -> 15.9 us  [to_near(): return lax.ppermute(value, BOTH, near_pairs)]
    ppermute x0 -> x2, waiting for transfers between devices: none -> 5.84 us  [all_parts(): return [value, a, b, lax.ppermute(value, BOTH, diag_pairs)]]
    ppermute x10 -> x8, waiting for transfers between devices: 11.5 us -> 6.6 us  [to_across(): return lax.ppermute(value, BOTH, across_pairs)]
    ppermute x0 -> x2, starting transfers between devices: none -> 4.37 us  [all_parts(): return [value, a, b, lax.ppermute(value, BOTH, diag_pairs)]]
    ppermute x10 -> x8, starting transfers between devices: 12.4 us -> 8.42 us  [to_across(): return lax.ppermute(value, BOTH, across_pairs)]
    ppermute x6, starting transfers between devices: 11 us -> 13.3 us  [to_near(): return lax.ppermute(value, BOTH, near_pairs)]
  transfers between devices with their start and end apart: 20 -> 20, of which waited for: 10 -> 11; matrix products, arithmetic and copies ran while one was open for 15% -> 16% of each run, Pallas kernels for 19% -> 19%
where the time goes in v4:
time: 222 us; the launch traced here: 219 us
  starting transfers between devices  65.7 us (30%)
  waiting for transfers between devices  61.3 us (28%)
  Pallas kernels  48.2 us (22%)
  matrix products  16.7 us (8%)
  other arithmetic  15.4 us (7%)
  between operations  7.82 us (4%)
  local copies, waits for them, and re-layouts  4.04 us (2%)
    pallas_call x4, Pallas kernels, half_ffn(): pl.pallas_call(ffn_kernel, out_shape=jax.ShapeDtypeStruct(x.shape, BF16),...  29.5 us
    all_to_all x2, starting transfers between devices, body(): returned = lax.all_to_all(out, 'ep', 0, 0, tiled=True)  21.5 us
    all_to_all x2, waiting for transfers between devices, body(): arrived = lax.all_to_all(there, 'ep', 0, 0, tiled=True)  21.3 us
    all_to_all x2, starting transfers between devices, body(): arrived = lax.all_to_all(there, 'ep', 0, 0, tiled=True)  18 us
    dot_general x12, matrix products, dot(): return lax.dot_general(a, b, (dims, ((), ())), preferred_element_type=F32)  16.7 us
    ppermute x6, waiting for transfers between devices, to_near(): return lax.ppermute(value, BOTH, near_pairs)  15.9 us
    ppermute x6, starting transfers between devices, to_near(): return lax.ppermute(value, BOTH, near_pairs)  13.3 us
    all_to_all x2, waiting for transfers between devices, body(): returned = lax.all_to_all(out, 'ep', 0, 0, tiled=True)  11.6 us
  transfers between devices with their start and end apart: 20, of which 11 were waited for; matrix products, arithmetic and copies ran while one was open for 16% of the time, Pallas kernels for 19%

profile of v4, /device:TPU:8, one launch (start us, length us, event | category | flops | bytes accessed | tf_op | source)
XLA Modules:
  0.0 219.1 jit_solution(8121437569746426337)
XLA Ops:
  9.3 5.8 %collective-permute-done.2.part_3 = bf16[256,512]{1,0:T(8,128)(2,1)} collective-permute-done((bf16[256,512]{1,0:T(8,128)(2,1)}, bf16[256,512]{1,0:T(8,128)(2,1)}, u32[]{:S(2)}, u32[]{:S(2)}) %collective-permute-start.2) | collective-permute-done | bytes 262176 | tf_op jit(solution)/shard_map/ppermute | solution.py:238
  15.2 3.0 %shard_map.112 = bf16[512,1024]{1,0:T(8,128)(2,1)} custom-call(s32[4]{0:T(128)} %add_multiply_fusion.starts, bf16[512,256]{1,0:T(8,128)(2,1)} %get-tuple-element.29.pick, bf16[256,512]{1,0:T(8,128)(2,1)} %part_0.3, bf16[256,512]{1,0:T(8,128)(2,1)} %copy-done.5, bf16[256,512]{1,0:T(8,128)(2,1)} %copy-done.6, bf16[256,512]{1,0:T(8,128)(2,1)} %collective-permute-done.2.part_3), custom_call_target="tpu_custom_call" | custom-call | flops 536870912 | bytes 2097152 | tf_op jit(solution)/shard_map/pallas_call | solution.py:145
  18.2 12.2 %all-to-all-start.2 = ((bf16[64,8,1024]{2,1,0:T(8,128)(2,1)}), bf16[64,8,1024]{2,1,0:T(8,128)(2,1)}, u32[]{:S(2)}, u32[]{:S(2)}) async-start(bf16[64,8,1024]{2,1,0:T(8,128)(2,1)} %bitcast.68), calls=%async_computation.2 | async-start | bytes 2097152 | tf_op jit(solution)/shard_map/all_to_all | solution.py:293
  34.3 3.4 %shard_map.109 = (bf16[512,1024]{1,0:T(8,128)(2,1)}, bf16[256,2048]{1,0:T(8,128)(2,1)}) custom-call(s32[4]{0:T(128)} %add_multiply_fusion.starts, bf16[512,256]{1,0:T(8,128)(2,1)} %get-tuple-element.30.pick, bf16[256,512]{1,0:T(8,128)(2,1)} %part_0.3, bf16[256,512]{1,0:T(8,128)(2,1)} %copy-done.5, bf16[256,512]{1,0:T(8,128)(2,1)} %copy-done.6, ...), custom_call_target="tpu_custom_call" | custom-call | flops 536870912 | bytes 2097152 | tf_op jit(solution)/shard_map/pallas_call | solution.py:145
  37.7 21.3 %all-to-all-done.2 = bf16[64,8,1024]{2,1,0:T(8,128)(2,1)} async-done(((bf16[64,8,1024]{2,1,0:T(8,128)(2,1)}), bf16[64,8,1024]{2,1,0:T(8,128)(2,1)}, u32[]{:S(2)}, u32[]{:S(2)}) %all-to-all-start.2) | async-done | bytes 1048608 | tf_op jit(solution)/shard_map/all_to_all | solution.py:293
  59.1 5.8 %all-to-all-start = ((bf16[64,8,1024]{2,1,0:T(8,128)(2,1)}), bf16[64,8,1024]{2,1,0:T(8,128)(2,1)}, u32[]{:S(2)}, u32[]{:S(2)}) async-start(bf16[64,8,1024]{2,1,0:T(8,128)(2,1)} %bitcast.69), calls=%async_computation | async-start | bytes 2097152 | tf_op jit(solution)/shard_map/all_to_all | solution.py:293
  64.9 3.0 %collective-permute-start.5 = (bf16[512,60]{0,1:T(8,128)(2,1)}, bf16[512,60]{0,1:T(8,128)(2,1)}, u32[]{:S(2)}, u32[]{:S(2)}) collective-permute-start(bf16[512,60]{0,1:T(8,128)(2,1)} %param.13), channel_id=1, source_target_pairs={{0,2},{1,3},{2,0},{3,1},{4,6},{5,7},{6,4},{7,5},{8,10},{9,11},{10,... | collective-permute-start | bytes 184328 | tf_op jit(solution)/shard_map/ppermute | solution.py:238
  81.8 10.5 %collective-permute-done.8.down_b = bf16[352,2048]{1,0:T(8,128)(2,1)} collective-permute-done((bf16[352,2048]{1,0:T(8,128)(2,1)}, bf16[352,2048]{1,0:T(8,128)(2,1)}, u32[]{:S(2)}, u32[]{:S(2)}) %collective-permute-start.8) | collective-permute-done | bytes 1441824 | tf_op jit(solution)/shard_map/ppermute | solution.py:231
  92.4 7.4 %shard_map.114 = bf16[512,1024]{1,0:T(8,128)(2,1)} custom-call(f32[1,2048]{1,0:T(1,128)} %bitcast.70, bf16[512,1024]{1,0:T(8,128)(2,1)} %collective-permute-done.11.x_in, bf16[352,2048]{1,0:T(8,128)(2,1)} %bitcast.54, bf16[352,2048]{1,0:T(8,128)(2,1)} %collective-permute-done.6.gate_b, bf16[352,2048]{1,0:T(8,128)(2,1)} %bitcast.59, ...), custom_call_target="tpu_custom_call" | custom-call | flops 2214592512 | bytes 10747904 | tf_op jit(solution)/shard_map/pallas_call | solution.py:106
  104.5 7.4 %shard_map.113 = bf16[512,1024]{1,0:T(8,128)(2,1)} custom-call(f32[1,2048]{1,0:T(1,128)} %bitcast.71, bf16[512,1024]{1,0:T(8,128)(2,1)} %bitcast.27.x_in, bf16[352,2048]{1,0:T(8,128)(2,1)} %bitcast.55, bf16[352,2048]{1,0:T(8,128)(2,1)} %collective-permute-done.6.gate_b, bf16[352,2048]{1,0:T(8,128)(2,1)} %bitcast.60, ...), custom_call_target="tpu_custom_call" | custom-call | flops 2214592512 | bytes 10747904 | tf_op jit(solution)/shard_map/pallas_call | solution.py:106
  111.9 3.1 %collective-permute-done.12 = bf16[512,1024]{1,0:T(8,128)(2,1)} collective-permute-done((bf16[512,1024]{1,0:T(8,128)(2,1)}, bf16[512,1024]{1,0:T(8,128)(2,1)}, u32[]{:S(2)}, u32[]{:S(2)}) %collective-permute-start.12) | collective-permute-done | bytes 1048608 | tf_op jit(solution)/shard_map/ppermute | solution.py:234
  115.0 2.9 %fusion.8 = bf16[64,8,1024]{2,1,0:T(8,128)(2,1)} fusion(bf16[512,1024]{1,0:T(8,128)(2,1)} %collective-permute-done.12, bf16[512,1024]{1,0:T(8,128)(2,1)} %shard_map.113), kind=kLoop, calls=%fused_computation.17 | loop fusion | flops 2097152 | bytes 3145728 | tf_op jit(solution)/shard_map/reshape | solution.py:299
  118.0 10.6 %all-to-all-start.3 = ((bf16[64,8,1024]{2,1,0:T(8,128)(2,1)}), bf16[64,8,1024]{2,1,0:T(8,128)(2,1)}, u32[]{:S(2)}, u32[]{:S(2)}) async-start(bf16[64,8,1024]{2,1,0:T(8,128)(2,1)} %fusion.8), calls=%async_computation.3 | async-start | bytes 2097152 | tf_op jit(solution)/shard_map/all_to_all | solution.py:300
  131.1 7.4 %shard_map.111 = bf16[512,1024]{1,0:T(8,128)(2,1)} custom-call(f32[1,2048]{1,0:T(1,128)} %bitcast.72, bf16[512,1024]{1,0:T(8,128)(2,1)} %collective-permute-done.9.x_in, bf16[352,2048]{1,0:T(8,128)(2,1)} %bitcast.56, bf16[352,2048]{1,0:T(8,128)(2,1)} %collective-permute-done.6.gate_b, bf16[352,2048]{1,0:T(8,128)(2,1)} %bitcast.61, ...), custom_call_target="tpu_custom_call" | custom-call | flops 2214592512 | bytes 10747904 | tf_op jit(solution)/shard_map/pallas_call | solution.py:106
  143.9 7.3 %shard_map.110 = bf16[512,1024]{1,0:T(8,128)(2,1)} custom-call(f32[1,2048]{1,0:T(1,128)} %bitcast.73, bf16[512,1024]{1,0:T(8,128)(2,1)} %bitcast.15.x_in, bf16[352,2048]{1,0:T(8,128)(2,1)} %bitcast.57, bf16[352,2048]{1,0:T(8,128)(2,1)} %collective-permute-done.6.gate_b, bf16[352,2048]{1,0:T(8,128)(2,1)} %bitcast.62, ...), custom_call_target="tpu_custom_call" | custom-call | flops 2214592512 | bytes 10747904 | tf_op jit(solution)/shard_map/pallas_call | solution.py:106
  153.8 2.7 %fusion.7 = bf16[64,8,1024]{2,1,0:T(8,128)(2,1)} fusion(bf16[512,1024]{1,0:T(8,128)(2,1)S(1)} %collective-permute-done.10, bf16[512,1024]{1,0:T(8,128)(2,1)} %shard_map.110), kind=kLoop, calls=%fused_computation.16 | loop fusion | flops 2097152 | bytes 3145728 | tf_op jit(solution)/shard_map/reshape | solution.py:299
  157.3 10.9 %all-to-all-start.1 = ((bf16[64,8,1024]{2,1,0:T(8,128)(2,1)}), bf16[64,8,1024]{2,1,0:T(8,128)(2,1)}, u32[]{:S(2)}, u32[]{:S(2)}) async-start(bf16[64,8,1024]{2,1,0:T(8,128)(2,1)} %fusion.7), calls=%async_computation.1 | async-start | bytes 2097152 | tf_op jit(solution)/shard_map/all_to_all | solution.py:300
  174.3 6.9 %convolution_multiply_fusion.base = f32[256,2048]{1,0:T(8,128)} fusion(bf16[704,2048]{1,0:T(8,128)(2,1)S(1)} %copy-done, f32[256]{0:T(256)S(1)} %add_divide_fusion, f32[256,704]{0,1:T(8,128)} %fusion.50, bf16[256,2048]{1,0:T(8,128)(2,1)} %fusion.2, bf16[2048,704]{0,1:T(8,128)(2,1)} %param.20), kind=kOutput, calls=%fused_computation | convolution fusion | flops 1478000640 | bytes 9634816 | tf_op jit(solution)/shard_map/dot_general | solution.py:31
  181.2 4.8 %shard_map.115.base = f32[256,2048]{1,0:T(8,128)} custom-call(bf16[2,256,512]{2,1,0:T(8,128)(2,1)} %get-tuple-element.19.mix_hi, bf16[2,256,512]{2,1,0:T(8,128)(2,1)} %get-tuple-element.20.mix_lo, bf16[512,1024]{1,0:T(8,128)(2,1)} %bitcast.29.rows, f32[256,2048]{1,0:T(8,128)} %convolution_multiply_fusion.base), custom_call_target="tpu_custom_call" | custom-call | flops 1073741824 | bytes 4194304 | tf_op jit(solution)/shard_map/pallas_call | solution.py:165
  186.1 10.8 %all-to-all-done.1 = bf16[64,8,1024]{2,1,0:T(8,128)(2,1)} async-done(((bf16[64,8,1024]{2,1,0:T(8,128)(2,1)}), bf16[64,8,1024]{2,1,0:T(8,128)(2,1)}, u32[]{:S(2)}, u32[]{:S(2)}) %all-to-all-start.1) | async-done | bytes 1048608 | tf_op jit(solution)/shard_map/all_to_all | solution.py:300
  196.9 3.7 %shard_map.117 = (bf16[256,512]{1,0:T(8,128)(2,1)}, bf16[256,512]{1,0:T(8,128)(2,1)}) custom-call(s32[4]{0:T(128)} %add_multiply_fusion.starts, bf16[2,256,512]{2,1,0:T(8,128)(2,1)} %get-tuple-element.16.mix_hi, bf16[2,256,512]{2,1,0:T(8,128)(2,1)} %get-tuple-element.17.mix_lo, bf16[512,1024]{1,0:T(8,128)(2,1)} %bitcast.24.rows, f32[256,2048]{1,0:T(8,128)} %shard_map.115.base), custom_call_target="tpu_custom_call" | custom-call | flops 536870912 | bytes 4194304 | tf_op jit(solution)/shard_map/pallas_call | solution.py:190
  202.6 3.8 %shard_map.116 = (f32[256,512]{1,0:T(8,128)}, f32[256,512]{1,0:T(8,128)}) custom-call(s32[4]{0:T(128)} %add_multiply_fusion.starts, bf16[2,256,512]{2,1,0:T(8,128)(2,1)} %get-tuple-element.16.mix_hi, bf16[2,256,512]{2,1,0:T(8,128)(2,1)} %get-tuple-element.17.mix_lo, bf16[512,1024]{1,0:T(8,128)(2,1)} %bitcast.24.rows, f32[256,2048]{1,0:T(8,128)} %shard_map.115.base), custom_call_target="tpu_custom_call" | custom-call | flops 536870912 | bytes 4194304 | tf_op jit(solution)/shard_map/pallas_call | solution.py:190
  208.3 5.7 %collective-permute-start.15 = (bf16[256,512]{1,0:T(8,128)(2,1)S(1)}, bf16[256,512]{1,0:T(8,128)(2,1)S(1)}, u32[]{:S(2)}, u32[]{:S(2)}) collective-permute-start(bf16[256,512]{1,0:T(8,128)(2,1)S(1)} %add_convert_fusion.3), channel_id=1, source_target_pairs={{0,1},{1,0},{2,3},{3,2},{4,7},{5,6},{6,5},{7,4},{8,9},{9,8},{10,11... | collective-permute-start | bytes 786440 | tf_op jit(solution)/shard_map/ppermute | solution.py:231
  215.1 3.2 %collective-permute-done.15 = bf16[256,512]{1,0:T(8,128)(2,1)S(1)} collective-permute-done((bf16[256,512]{1,0:T(8,128)(2,1)S(1)}, bf16[256,512]{1,0:T(8,128)(2,1)S(1)}, u32[]{:S(2)}, u32[]{:S(2)}) %collective-permute-start.15) | collective-permute-done | bytes 262176 | tf_op jit(solution)/shard_map/ppermute | solution.py:231
  (85 shorter events, 47.4 us)
Async XLA Ops:
  0.0 174.3 %copy-start = (bf16[704,2048]{1,0:T(8,128)(2,1)S(1)}, bf16[704,2048]{1,0:T(8,128)(2,1)}, u32[]{:S(2)}) copy-start(bf16[704,2048]{1,0:T(8,128)(2,1)} %param.21) | copy-start | bytes 8650756
  0.0 9.3 %collective-permute-start = (bf16[256,512]{1,0:T(8,128)(2,1)}, bf16[256,512]{1,0:T(8,128)(2,1)S(1)}, u32[]{:S(2)}, u32[]{:S(2)}) collective-permute-start(bf16[256,512]{1,0:T(8,128)(2,1)} %part_0.3), channel_id=1, source_target_pairs={{0,1},{1,0},{2,3},{3,2},{4,7},{5,6},{6,5},{7,4},{8,9},{9,8},{10,11... | collective-permute-start | bytes 786440 | tf_op jit(solution)/shard_map/ppermute | solution.py:231
  2.2 7.2 %collective-permute-start.1 = (bf16[256,512]{1,0:T(8,128)(2,1)}, bf16[256,512]{1,0:T(8,128)(2,1)S(1)}, u32[]{:S(2)}, u32[]{:S(2)}) collective-permute-start(bf16[256,512]{1,0:T(8,128)(2,1)} %part_0.3), channel_id=1, source_target_pairs={{0,3},{1,2},{2,1},{3,0},{4,5},{5,4},{6,7},{7,6},{8,11},{9,10},{10,... | collective-permute-start | bytes 786440 | tf_op jit(solution)/shard_map/ppermute | solution.py:234
  2.9 12.3 %collective-permute-start.2 = (bf16[256,512]{1,0:T(8,128)(2,1)}, bf16[256,512]{1,0:T(8,128)(2,1)}, u32[]{:S(2)}, u32[]{:S(2)}) collective-permute-start(bf16[256,512]{1,0:T(8,128)(2,1)} %part_0.3), channel_id=1, source_target_pairs={{0,2},{1,3},{2,0},{3,1},{4,6},{5,7},{6,4},{7,5},{8,10},{9,11},{10,... | collective-permute-start | bytes 786440 | tf_op jit(solution)/shard_map/ppermute | solution.py:238
  18.2 40.9 %all-to-all-start.2 = ((bf16[64,8,1024]{2,1,0:T(8,128)(2,1)}), bf16[64,8,1024]{2,1,0:T(8,128)(2,1)}, u32[]{:S(2)}, u32[]{:S(2)}) async-start(bf16[64,8,1024]{2,1,0:T(8,128)(2,1)} %bitcast.68), calls=%async_computation.2 | async-start | bytes 2097152 | tf_op jit(solution)/shard_map/all_to_all | solution.py:293
  30.4 37.9 %copy-start.8 = (s32[4]{0:T(128)S(1)}, s32[4]{0:T(128)}, u32[]{:S(2)}) copy-start(s32[4]{0:T(128)} %add_multiply_fusion.starts) | copy-start | bytes 52
  30.4 43.6 %copy-start.9 = (bf16[2048]{0:T(1024)(128)(2,1)S(1)}, bf16[2048]{0:T(1024)(128)(2,1)}, u32[]{:S(2)}) copy-start(bf16[2048]{0:T(1024)(128)(2,1)} %param.14) | copy-start | bytes 12292
  30.4 48.8 %collective-permute-start.6 = (bf16[352,2048]{1,0:T(8,128)(2,1)}, bf16[352,2048]{1,0:T(8,128)(2,1)}, u32[]{:S(2)}, u32[]{:S(2)}) collective-permute-start(bf16[352,2048]{1,0:T(8,128)(2,1)} %bitcast.53), channel_id=1, source_target_pairs={{0,1},{1,0},{2,3},{3,2},{4,7},{5,6},{6,5},{7,4},{8,9},{9,8},{10,11... | collective-permute-start | bytes 4325384 | tf_op jit(solution)/shard_map/ppermute | solution.py:231
  32.3 48.4 %collective-permute-start.7 = (bf16[352,2048]{1,0:T(8,128)(2,1)}, bf16[352,2048]{1,0:T(8,128)(2,1)}, u32[]{:S(2)}, u32[]{:S(2)}) collective-permute-start(bf16[352,2048]{1,0:T(8,128)(2,1)} %bitcast.58), channel_id=1, source_target_pairs={{0,1},{1,0},{2,3},{3,2},{4,7},{5,6},{6,5},{7,4},{8,9},{9,8},{10,11... | collective-permute-start | bytes 4325384 | tf_op jit(solution)/shard_map/ppermute | solution.py:231
  32.5 59.8 %collective-permute-start.8 = (bf16[352,2048]{1,0:T(8,128)(2,1)}, bf16[352,2048]{1,0:T(8,128)(2,1)}, u32[]{:S(2)}, u32[]{:S(2)}) collective-permute-start(bf16[352,2048]{1,0:T(8,128)(2,1)} %bitcast.63), channel_id=1, source_target_pairs={{0,1},{1,0},{2,3},{3,2},{4,7},{5,6},{6,5},{7,4},{8,9},{9,8},{10,11... | collective-permute-start | bytes 4325384 | tf_op jit(solution)/shard_map/ppermute | solution.py:231
  59.1 44.2 %all-to-all-start = ((bf16[64,8,1024]{2,1,0:T(8,128)(2,1)}), bf16[64,8,1024]{2,1,0:T(8,128)(2,1)}, u32[]{:S(2)}, u32[]{:S(2)}) async-start(bf16[64,8,1024]{2,1,0:T(8,128)(2,1)} %bitcast.69), calls=%async_computation | async-start | bytes 2097152 | tf_op jit(solution)/shard_map/all_to_all | solution.py:293
  64.9 38.4 %collective-permute-start.5 = (bf16[512,60]{0,1:T(8,128)(2,1)}, bf16[512,60]{0,1:T(8,128)(2,1)}, u32[]{:S(2)}, u32[]{:S(2)}) collective-permute-start(bf16[512,60]{0,1:T(8,128)(2,1)} %param.13), channel_id=1, source_target_pairs={{0,2},{1,3},{2,0},{3,1},{4,6},{5,7},{6,4},{7,5},{8,10},{9,11},{10,... | collective-permute-start | bytes 184328 | tf_op jit(solution)/shard_map/ppermute | solution.py:238
  67.9 24.4 %collective-permute-start.11 = (bf16[512,1024]{1,0:T(8,128)(2,1)}, bf16[512,1024]{1,0:T(8,128)(2,1)}, u32[]{:S(2)}, u32[]{:S(2)}) collective-permute-start(bf16[512,1024]{1,0:T(8,128)(2,1)} %bitcast.27.x_in), channel_id=1, source_target_pairs={{0,3},{1,2},{2,1},{3,0},{4,5},{5,4},{6,7},{7,6},{8,11},{9,10},{10,... | collective-permute-start | bytes 3145736 | tf_op jit(solution)/shard_map/ppermute | solution.py:234
  79.2 49.4 %collective-permute-start.3 = (bf16[512,60]{0,1:T(8,128)(2,1)}, bf16[512,60]{0,1:T(8,128)(2,1)S(1)}, u32[]{:S(2)}, u32[]{:S(2)}) collective-permute-start(bf16[512,60]{0,1:T(8,128)(2,1)} %param.13), channel_id=1, source_target_pairs={{0,1},{1,0},{2,3},{3,2},{4,7},{5,6},{6,5},{7,4},{8,9},{9,8},{10,11... | collective-permute-start | bytes 184328 | tf_op jit(solution)/shard_map/ppermute | solution.py:231
  80.7 59.9 %collective-permute-start.4 = (bf16[512,60]{0,1:T(8,128)(2,1)}, bf16[512,60]{0,1:T(8,128)(2,1)}, u32[]{:S(2)}, u32[]{:S(2)}) collective-permute-start(bf16[512,60]{0,1:T(8,128)(2,1)} %param.13), channel_id=1, source_target_pairs={{0,3},{1,2},{2,1},{3,0},{4,5},{5,4},{6,7},{7,6},{8,11},{9,10},{10,... | collective-permute-start | bytes 184328 | tf_op jit(solution)/shard_map/ppermute | solution.py:234
  99.8 15.2 %collective-permute-start.12 = (bf16[512,1024]{1,0:T(8,128)(2,1)}, bf16[512,1024]{1,0:T(8,128)(2,1)}, u32[]{:S(2)}, u32[]{:S(2)}) collective-permute-start(bf16[512,1024]{1,0:T(8,128)(2,1)} %shard_map.114), channel_id=1, source_target_pairs={{0,3},{1,2},{2,1},{3,0},{4,5},{5,4},{6,7},{7,6},{8,11},{9,10},{10,... | collective-permute-start | bytes 3145736 | tf_op jit(solution)/shard_map/ppermute | solution.py:234
  103.2 27.9 %collective-permute-start.9 = (bf16[512,1024]{1,0:T(8,128)(2,1)}, bf16[512,1024]{1,0:T(8,128)(2,1)}, u32[]{:S(2)}, u32[]{:S(2)}) collective-permute-start(bf16[512,1024]{1,0:T(8,128)(2,1)} %bitcast.15.x_in), channel_id=1, source_target_pairs={{0,3},{1,2},{2,1},{3,0},{4,5},{5,4},{6,7},{7,6},{8,11},{9,10},{10,... | collective-permute-start | bytes 3145736 | tf_op jit(solution)/shard_map/ppermute | solution.py:234
  118.0 39.3 %all-to-all-start.3 = ((bf16[64,8,1024]{2,1,0:T(8,128)(2,1)}), bf16[64,8,1024]{2,1,0:T(8,128)(2,1)}, u32[]{:S(2)}, u32[]{:S(2)}) async-start(bf16[64,8,1024]{2,1,0:T(8,128)(2,1)} %fusion.8), calls=%async_computation.3 | async-start | bytes 2097152 | tf_op jit(solution)/shard_map/all_to_all | solution.py:300
  138.5 15.3 %collective-permute-start.10 = (bf16[512,1024]{1,0:T(8,128)(2,1)}, bf16[512,1024]{1,0:T(8,128)(2,1)S(1)}, u32[]{:S(2)}, u32[]{:S(2)}) collective-permute-start(bf16[512,1024]{1,0:T(8,128)(2,1)} %shard_map.111), channel_id=1, source_target_pairs={{0,3},{1,2},{2,1},{3,0},{4,5},{5,4},{6,7},{7,6},{8,11},{9,10},{10,... | collective-permute-start | bytes 3145736 | tf_op jit(solution)/shard_map/ppermute | solution.py:234
  156.5 11.7 %copy-start.4 = (bf16[256,512]{1,0:T(8,128)(2,1)S(1)}, bf16[256,512]{1,0:T(8,128)(2,1)}, u32[]{:S(2)}) copy-start(bf16[256,512]{1,0:T(8,128)(2,1)} %fusion.23) | copy-start | bytes 786436
  157.3 39.6 %all-to-all-start.1 = ((bf16[64,8,1024]{2,1,0:T(8,128)(2,1)}), bf16[64,8,1024]{2,1,0:T(8,128)(2,1)}, u32[]{:S(2)}, u32[]{:S(2)}) async-start(bf16[64,8,1024]{2,1,0:T(8,128)(2,1)} %fusion.7), calls=%async_computation.1 | async-start | bytes 2097152 | tf_op jit(solution)/shard_map/all_to_all | solution.py:300
  200.6 6.6 %collective-permute-start.14 = (bf16[256,512]{1,0:T(8,128)(2,1)}, bf16[256,512]{1,0:T(8,128)(2,1)S(1)}, u32[]{:S(2)}, u32[]{:S(2)}) collective-permute-start(bf16[256,512]{1,0:T(8,128)(2,1)} %get-tuple-element.24), channel_id=1, source_target_pairs={{0,3},{1,2},{2,1},{3,0},{4,5},{5,4},{6,7},{7,6},{8,11},{9,10},{10,... | collective-permute-start | bytes 786440 | tf_op jit(solution)/shard_map/ppermute | solution.py:234
  202.5 11.5 %collective-permute-start.13 = (bf16[256,512]{1,0:T(8,128)(2,1)}, bf16[256,512]{1,0:T(8,128)(2,1)S(1)}, u32[]{:S(2)}, u32[]{:S(2)}) collective-permute-start(bf16[256,512]{1,0:T(8,128)(2,1)} %get-tuple-element.22), channel_id=1, source_target_pairs={{0,3},{1,2},{2,1},{3,0},{4,5},{5,4},{6,7},{7,6},{8,11},{9,10},{10,... | collective-permute-start | bytes 786440 | tf_op jit(solution)/shard_map/ppermute | solution.py:234
  208.3 10.0 %collective-permute-start.15 = (bf16[256,512]{1,0:T(8,128)(2,1)S(1)}, bf16[256,512]{1,0:T(8,128)(2,1)S(1)}, u32[]{:S(2)}, u32[]{:S(2)}) collective-permute-start(bf16[256,512]{1,0:T(8,128)(2,1)S(1)} %add_convert_fusion.3), channel_id=1, source_target_pairs={{0,1},{1,0},{2,3},{3,2},{4,7},{5,6},{6,5},{7,4},{8,9},{9,8},{10,11... | collective-permute-start | bytes 786440 | tf_op jit(solution)/shard_map/ppermute | solution.py:231
  (7 other events, 47.2 us)
